TPU v7x, 32 devices: a whole 2x2x4 slice. The times are simulated.
32 devices in a mesh: gx: 16 (over z, y, core), gy: 2 (over x).
Axes of the slice: x: 2, y: 2, z: 4, core: 2. Of those that a mesh axis runs over, the one named last changes fastest.
Arguments:
- old_block: float32 [12288, 24576], P('gx', 'gy'), may hold values from -6 to 6
- vectors: bfloat16 [256, 2, 12288], P(None, 'gy', 'gx'), may hold values from -4 to 4
- prior: bfloat16 [32768, 3072], P('gx', 'gy'), may hold values from -2 to 2
- pair_columns: float32 [32768, 128], P(('gx', 'gy')), may hold values from -6 to 6
- pivots: int32 [128], replicated, may hold values from 0 to 32767
Outputs:
- new_block: float32 [12288, 24576], P('gx', 'gy')
- residual_columns: float32 [32768, 128], P(('gx', 'gy'))
Inputs may be any that keep to these rules, and one draw needn't show every extreme that they name: `pivots`: pivot AO-pair row indices, repeats possible.
All inputs are finite; a program needn't handle non-finite values.
Results may differ from a plain program's by a relative error of at most 0.0055.
Values may be sent and summed in bfloat16 or wider, within the bound.
No kernel may reach another device: no remote copies, remote signals or barrier semaphores. Data moves between devices by JAX's collectives and lax.ppermute only.
A program may use at most 192 MiB of HBM per device.

v0:
```python
import jax
import jax.numpy as jnp
from jax import lax
from jax.sharding import PartitionSpec as P


def from_root(value, axis, root):
    mine = lax.axis_index(axis) == root
    return lax.psum(jnp.where(mine, value, jnp.zeros_like(value)), axis)


def local(old_block, vectors, prior, pair_columns, pivots):
    local_vectors = vectors.reshape(vectors.shape[0], vectors.shape[2])
    slab_part = from_root(local_vectors, "gy", 0)
    gained = jnp.dot(
        slab_part.T,
        lax.all_gather(local_vectors, "gx", axis=1, tiled=True),
        preferred_element_type=jnp.float32,
    )
    new_block = old_block + gained
    rows_local = prior.shape[0]
    offset = lax.axis_index("gx") * rows_local
    local_index = pivots - offset
    inside = jnp.logical_and(local_index >= 0, local_index < rows_local)
    chosen = jnp.take(prior, jnp.clip(local_index, 0, rows_local - 1), axis=0).astype(jnp.float32)
    chosen = chosen * inside[:, None].astype(jnp.float32)
    pivot_block = lax.psum(chosen.astype(jnp.bfloat16), "gx")
    groups = lax.axis_size("gy")
    width = prior.shape[1]
    regrouped = lax.all_to_all(prior, "gy", split_axis=0, concat_axis=1, tiled=True)
    full_pivots = lax.all_gather(pivot_block, "gy", axis=1, tiled=True)
    parts = jnp.einsum(
        "rgc,kgc->grk",
        regrouped.reshape(regrouped.shape[0], groups, width),
        full_pivots.reshape(full_pivots.shape[0], groups, width),
        preferred_element_type=jnp.float32,
    )
    rounded = lax.optimization_barrier(parts.astype(jnp.bfloat16))
    intersection = jnp.sum(rounded.astype(jnp.float32), axis=0)
    return (new_block, pair_columns - intersection)


def solution(mesh):
    placed = (P("gx", "gy"), P(None, "gy", "gx"), P("gx", "gy"), P(("gx", "gy"), None), P())
    return jax.shard_map(
        local,
        mesh=mesh,
        in_specs=placed,
        out_specs=(P("gx", "gy"), P(("gx", "gy"), None)),
        check_vma=False,
    )
```

profile of v0, /device:TPU:0, one launch (start us, length us, event | category | flops | bytes accessed | tf_op | source)
XLA Modules:
  0.0 236.3 jit_solution(9439408910341760958)
XLA Ops:
  7.2 0.0 all-reduce.5.cloned.1.call-start
  7.2 0.7 compare_and_fusion
  7.9 4.8 %gather_fusion = bf16[128,1536]{1,0:T(8,128)(2,1)S(1)} fusion(bf16[2048,1536]{1,0:T(8,128)(2,1)} %param.7, s32[1024]{0:T(1024)S(1)} %pad_clamp_fusion), kind=kCustom, calls=%fused_computation | custom fusion | bytes 786944 | tf_op jit(solution)/shard_map/jit(_take)/gather | solution.py:25
  12.7 0.9 multiply_convert_fusion
  13.7 0.0 all-reduce.5.cloned.1.call-update
  13.7 0.0 all-reduce.3.cloned.1.call-start
  13.8 1.8 select_bitcast_fusion
  15.6 0.0 all-reduce.3.cloned.1.call-update
  15.6 0.0 all-gather.3.cloned.1.call-start
  15.6 0.7 all-gather.3.cloned.1.call-update
  16.3 0.0 copy-start
  16.3 6.5 %all-to-all-start = ((bf16[2,1024,1536]{2,1,0:T(8,128)(2,1)}), bf16[2,1024,1536]{2,1,0:T(8,128)(2,1)}, u32[]{:S(2)}, u32[]{:S(2)}) async-start(bf16[2,1024,1536]{2,1,0:T(8,128)(2,1)} %bitcast.18), calls=%async_computation | async-start | bytes 12582912 | tf_op jit(solution)/shard_map/all_to_all | solution.py:30
  22.8 0.0 copy-done
  22.8 0.2 copy.11
  23.0 84.9 %all-reduce.5.cloned.1.call-done = bf16[128,1536]{1,0:T(8,128)(2,1)} async-done(((bf16[128,1536]{1,0:T(8,128)(2,1)}), bf16[128,1536]{1,0:T(8,128)(2,1)}) %all-reduce.5.cloned.1.call-update) | async-done | bytes 393232 | tf_op jit(solution)/shard_map/psum | solution.py:27
  107.9 14.1 %all_gather.7 = bf16[128,3072]{1,0:T(8,128)(2,1)S(1)} all-gather(bf16[128,1536]{1,0:T(8,128)(2,1)} %all-reduce.5.cloned.1.call-done), channel_id=1, replica_groups=mesh['gx'=16,'gy'=2] {'gy'}, dimensions={1}, use_global_device_ids=true | all-gather | bytes 1179648 | tf_op jit(solution)/shard_map/all_gather | solution.py:31
  122.1 0.4 copy.9
  122.4 0.0 all-to-all-done
  122.4 5.0 %fusion.6 = bf16[2,1024,128]{1,2,0:T(8,128)(2,1)S(1)} fusion(bf16[128,2,1536]{0,2,1:T(8,128)(2,1)S(1)} %bitcast.19, bf16[2,1024,1536]{2,1,0:T(8,128)(2,1)} %all-to-all-done), kind=kOutput, calls=%fused_computation.6 | convolution fusion | flops 805568512 | bytes 7602176 | tf_op jit(solution)/shard_map/rgc,kgc->grk/dot_general | solution.py:32
  127.5 0.1 convert_reduce_fusion
  127.6 0.1 sub.11
  127.6 1.0 copy.12
  128.6 7.6 %all-reduce.3.cloned.1.call-done = bf16[256,768]{1,0:T(8,128)(2,1)} async-done(((bf16[256,768]{1,0:T(8,128)(2,1)}), bf16[256,768]{1,0:T(8,128)(2,1)}) %all-reduce.3.cloned.1.call-update) | async-done | bytes 393232 | tf_op jit(solution)/shard_map/psum | solution.py:9
  136.2 63.9 %all-gather.3.cloned.1.call-done = bf16[256,1,12288]{2,0,1:T(8,128)(2,1)} async-done(((bf16[256,1,768]{2,0,1:T(8,128)(2,1)}), bf16[256,1,12288]{2,0,1:T(8,128)(2,1)}) %all-gather.3.cloned.1.call-update) | async-done | bytes 6291472 | tf_op jit(solution)/shard_map/all_gather | solution.py:17
  200.1 29.6 %convolution_add_fusion = f32[768,12288]{1,0:T(8,128)} fusion(f32[768,12288]{1,0:T(8,128)} %param.5, bf16[256,768]{1,0:T(8,128)(2,1)} %all-reduce.3.cloned.1.call-done, bf16[256,1,12288]{2,0,1:T(8,128)(2,1)} %all-gather.3.cloned.1.call-done), kind=kOutput, calls=%fused_computation.1 | convolution fusion | flops 4841275392 | bytes 82182144 | tf_op jit(solution)/shard_map/dot_general | solution.py:15
  (1 shorter events, 0.0 us)
Async XLA Ops:
  7.2 100.7 %all-reduce.5.cloned.1.call-start = ((), (), s32[]{:S(2)}) async-start(), calls=%async_computation.2 | async-start | bytes 786432 | tf_op jit(solution)/shard_map/psum | solution.py:27
  13.7 122.5 %all-reduce.3.cloned.1.call-start = ((), (), s32[]{:S(2)}) async-start(), calls=%async_computation.1 | async-start | bytes 786432 | tf_op jit(solution)/shard_map/psum | solution.py:9
  15.6 184.5 %all-gather.3.cloned.1.call-start = ((), (), s32[]{:S(2)}) async-start(), calls=%async_computation.3 | async-start | bytes 6684672 | tf_op jit(solution)/shard_map/all_gather | solution.py:17
  16.3 6.5 %copy-start = (f32[1024,128]{1,0:T(8,128)S(1)}, f32[1024,128]{1,0:T(8,128)}, u32[]{:S(2)}) copy-start(f32[1024,128]{1,0:T(8,128)} %param.8) | copy-start | bytes 1572868
  16.3 106.1 %all-to-all-start = ((bf16[2,1024,1536]{2,1,0:T(8,128)(2,1)}), bf16[2,1024,1536]{2,1,0:T(8,128)(2,1)}, u32[]{:S(2)}, u32[]{:S(2)}) async-start(bf16[2,1024,1536]{2,1,0:T(8,128)(2,1)} %bitcast.18), calls=%async_computation | async-start | bytes 12582912 | tf_op jit(solution)/shard_map/all_to_all | solution.py:30
Sparse Core Ops, SparseCore 0:
  13.8 94.0 all-reduce.4
  110.8 25.4 all-reduce.2
  138.5 61.5 all-gather.2
where the time goes:
time: 237 us; the launch traced here: 236 us
  waiting for transfers between devices  157 us (66%)
  matrix products  34.7 us (15%)
  blocking collectives  14.1 us (6%)
  between operations  13.8 us (6%)
  starting transfers between devices  6.59 us (3%)
  local copies, waits for them, and re-layouts  6.42 us (3%)
  other arithmetic  3.57 us (2%)
    psum x1, waiting for transfers between devices, local(): pivot_block = lax.psum(chosen.astype(jnp.bfloat16), 'gx')  84.9 us
    all_gather x1, waiting for transfers between devices, local(): lax.all_gather(local_vectors, 'gx', axis=1, tiled=True)  63.9 us
    dot_general x1, matrix products, local(): jnp.dot(slab_part.T, lax.all_gather(local_vectors, 'gx', axis=1, tiled=Tr...  29.6 us
    all_gather x1, blocking collectives, local(): full_pivots = lax.all_gather(pivot_block, 'gy', axis=1, tiled=True)  14.1 us
    psum x1, waiting for transfers between devices, from_root(): return lax.psum(jnp.where(mine, value, jnp.zeros_like(value)), axis)  7.58 us
    all_to_all x1, starting transfers between devices, local(): lax.all_to_all(prior, 'gy', split_axis=0, concat_axis=1, tiled=True)  6.47 us
    dot_general x1, matrix products, local(): jnp.einsum('rgc,kgc->grk', regrouped.reshape(regrouped.shape[0], groups,...  5.02 us
    gather x1, local copies, waits for them, and re-layouts, local(): jnp.take(prior, jnp.clip(local_index, 0, rows_local - 1), axis=0)  4.85 us
  transfers between devices with their start and end apart: 4, of which 3 were waited for; matrix products, arithmetic and copies ran while one was open for 4% of the time, Pallas kernels for 0%

commit v1 on v0

v1 whole, which is shorter than its diff:
```python
import functools

import jax
import jax.numpy as jnp
from jax import lax
from jax.experimental import pallas as pl
from jax.experimental.pallas import tpu as pltpu
from jax.sharding import PartitionSpec as P


def factors(n):
    core = 2 if n % 2 == 0 else 1
    near = 2 if (n // core) % 2 == 0 else 1
    return n // (core * near), near, core


HBM = pl.BlockSpec(memory_space=pltpu.HBM)
VMEM = pl.BlockSpec(memory_space=pltpu.VMEM)
SMEM = pl.BlockSpec(memory_space=pltpu.SMEM)


def keep(x):
    return pltpu.with_memory_space_constraint(x, pltpu.HBM)


def call(kernel, out_shape, operands, specs, out_specs, scratch=(), aliases=None, limit=8, flops=0):
    return pl.pallas_call(
        kernel,
        out_shape=out_shape,
        in_specs=specs,
        out_specs=out_specs,
        scratch_shapes=list(scratch),
        input_output_aliases=aliases or {},
        compiler_params=pltpu.CompilerParams(vmem_limit_bytes=limit * 1024 * 1024),
        cost_estimate=pl.CostEstimate(flops=flops, bytes_accessed=0, transcendentals=0),
    )(*operands)


def update_kernel(me, *rest, spots, extent, tiles, first):
    far, near, cores = extent
    count = len(spots)
    held, arrive, leave = rest[-3:]
    high, width = held.shape[1:]
    z, y, c = me[0] // (near * cores), me[0] // cores % near, me[0] % cores
    pieces = [(at, tile) for at in range(count) for tile in range(tiles)]
    if first:
        mask, own, got, *blocks = rest[: count + 2]
        old, out, slab, mine, here = rest[count + 2 : count + 7]
        blocks = [mine, *blocks]
    else:
        slab, *blocks = rest[: count + 1]
        old, out = rest[count + 1], rest[-4]

    def spot(at, tile):
        a, b, d = spots[at]
        column = (((z + a + far) % far * near) + (y + b) % near) * cores + (c + d) % cores
        return pl.ds(tile * high, high), pl.ds(pl.multiple_of(column * width, 128), width)

    def load(n):
        return pltpu.make_async_copy(old.at[spot(*pieces[n])], held.at[n], arrive.at[n])

    def save(n):
        return pltpu.make_async_copy(held.at[n], out.at[spot(*pieces[n])], leave.at[n])

    if first:
        bring = pltpu.make_async_copy(own, mine, here)
        bring.start()
    for n in range(len(pieces)):
        load(n).start()
    if first:
        bring.wait()
        chosen = jnp.where(mask[0] != 0, got[...].astype(jnp.float32), mine[...].astype(jnp.float32))
        slab[...] = chosen.T.astype(slab.dtype)
    for n, (at, tile) in enumerate(pieces):
        load(n).wait()
        held[n] += jnp.dot(
            slab[tile * high : (tile + 1) * high, :], blocks[at][...], preferred_element_type=jnp.float32
        )
        save(n).start()
    for n in range(len(pieces)):
        save(n).wait()


def update(me, rows_of, old, blocks, spots, extent, target):
    first = target is None
    inner, width = blocks[-1].shape
    rows = old.shape[0]
    count = len(blocks)
    tiles = next(t for t in (3, 2, 1) if rows % (8 * t) == 0)
    high = rows // tiles
    shape = jax.ShapeDtypeStruct(old.shape, old.dtype)
    scratch = [
        pltpu.VMEM((count * tiles, high, width), old.dtype),
        pltpu.SemaphoreType.DMA((count * tiles,)),
        pltpu.SemaphoreType.DMA((count * tiles,)),
    ]
    if first:
        mask, got = rows_of
        operands = [me, mask, keep(blocks[0]), got, *blocks[1:], keep(old)]
        specs = [SMEM, SMEM, HBM, VMEM] + [VMEM] * (count - 1) + [HBM]
        aliases = {}
        outs = [shape, jax.ShapeDtypeStruct((rows, inner), got.dtype)]
        out_specs = [HBM, VMEM]
        scratch = [pltpu.VMEM((inner, width), got.dtype), pltpu.SemaphoreType.DMA] + scratch
    else:
        operands = [me, rows_of, *blocks, keep(old), target]
        specs = [SMEM, VMEM] + [VMEM] * count + [HBM, HBM]
        aliases = {len(operands) - 1: 0}
        outs, out_specs = shape, HBM
    return call(
        functools.partial(update_kernel, spots=spots, extent=extent, tiles=tiles, first=first),
        outs,
        operands,
        specs,
        out_specs,
        scratch=scratch,
        aliases=aliases,
        limit=16,
        flops=2 * rows * inner * width * count,
    )


def add_kernel(a, b, out):
    out[...] = a[...] + b[...]


def add(a, b):
    return call(add_kernel, jax.ShapeDtypeStruct(a.shape, a.dtype), [a, b], [VMEM, VMEM], VMEM)


def pick_kernel(pivots, me, prior, kept, sent, tiles, total, owned, spots, arrive, *, cores):
    count = pivots.shape[0]
    rows = prior.shape[0]
    base = me[0] * rows

    def list_owned(k, found):
        row = pivots[k] - base
        owned[found] = k
        spots[found] = row
        return found + jnp.where(jnp.logical_and(row >= 0, row < rows), 1, 0)

    found = lax.fori_loop(0, count, list_owned, 0, unroll=8)

    def copy(n):
        start = pl.multiple_of(spots[n] // 8 * 8, 8)
        return pltpu.make_async_copy(prior.at[pl.ds(start, 8), :], tiles.at[n], arrive)

    def begin(n, carry):
        copy(n).start()
        return carry

    lax.fori_loop(0, found, begin, 0)
    total[...] = jnp.zeros_like(total)

    def finish(n, carry):
        copy(n).wait()
        return carry

    lax.fori_loop(0, found, finish, 0)

    def place(n, carry):
        tile = tiles[n].astype(jnp.float32)
        at = lax.broadcasted_iota(jnp.int32, tile.shape, 0)
        row = jnp.sum(jnp.where(at == spots[n] % 8, tile, 0.0), axis=0, keepdims=True)
        total[pl.ds(owned[n], 1), :] = row
        return carry

    lax.fori_loop(0, found, place, 0)
    half = count // cores
    c = me[0] % cores
    kept[...] = total[pl.ds(pl.multiple_of(c * half, 8), half), :].astype(kept.dtype)
    if cores > 1:
        sent[...] = total[pl.ds(pl.multiple_of((1 - c) * half, 8), half), :].astype(sent.dtype)


def pick(pivots, me, prior, cores):
    count = pivots.shape[0]
    width = prior.shape[1]
    shape = jax.ShapeDtypeStruct((count // cores, width), prior.dtype)
    return call(
        functools.partial(pick_kernel, cores=cores),
        [shape, shape],
        [pivots, me, keep(prior)],
        [SMEM, SMEM, HBM],
        [VMEM, VMEM],
        scratch=[
            pltpu.VMEM((count, 8, width), prior.dtype),
            pltpu.VMEM((count, width), jnp.float32),
            pltpu.SMEM((count + 8,), jnp.int32),
            pltpu.SMEM((count + 8,), jnp.int32),
            pltpu.SemaphoreType.DMA,
        ],
        limit=5,
    )


def parts_kernel(me, mine, *rest, cores, groups):
    prior, kept = rest[0], rest[1]
    outs = rest[1 + cores : 1 + cores + groups]
    picked = rest[-1]
    height = outs[0].shape[0]
    half = kept.shape[0]
    c = me[0] % cores
    picked[pl.ds(pl.multiple_of(c * half, 8), half), :] = kept[...]
    if cores > 1:
        picked[pl.ds(pl.multiple_of((1 - c) * half, 8), half), :] = rest[2][...]
    for g in range(groups):
        start = (mine[0] + 1 + g) % groups * height
        outs[g][...] = lax.dot_general(
            prior[pl.ds(pl.multiple_of(start, 8), height), :],
            picked[...],
            (((1,), (1,)), ((), ())),
            preferred_element_type=jnp.float32,
        ).astype(outs[g].dtype)


def parts_of(me, mine, prior, picked, cores, groups):
    rows, width = prior.shape
    count = picked[0].shape[0] * cores
    height = rows // groups
    return call(
        functools.partial(parts_kernel, cores=cores, groups=groups),
        [jax.ShapeDtypeStruct((height, count), prior.dtype)] * groups,
        [me, mine, prior, *picked],
        [SMEM, SMEM, VMEM] + [VMEM] * cores,
        [VMEM] * groups,
        scratch=[pltpu.VMEM((count, width), prior.dtype)],
        limit=16,
    )


def local(old_block, vectors, prior, pair_columns, pivots):
    size = lax.axis_size("gx")
    groups = lax.axis_size("gy")
    far, near, cores = factors(size)
    me = lax.axis_index("gx")
    mine = lax.axis_index("gy")
    everyone = [(a, b, d) for a in range(far) for b in range(near) for d in range(cores)]

    def place(a, b, d):
        return (a % far * near + b % near) * cores + d % cores

    def shift(x, a=0, b=0, d=0):
        return lax.ppermute(x, "gx", [(place(i, j, k), place(i + a, j + b, k + d)) for i, j, k in everyone])

    def swap_far(x, bit):
        return lax.ppermute(x, "gx", [(place(i, j, k), place(i ^ bit, j, k)) for i, j, k in everyone])

    own = vectors.reshape(vectors.shape[0], vectors.shape[2])
    width = own.shape[1]
    tiled = width % 128 == 0

    lines = [(own, 0)]
    forward = backward = own
    if tiled:
        for step in range(1, far // 2 + 1):
            forward = shift(forward, a=1)
            lines.append((forward, -step))
            if step < far - far // 2:
                backward = shift(backward, a=-1)
                lines.append((backward, step))

    slab = own
    reach = 1
    while reach < groups:
        got = lax.ppermute(slab, "gy", [(g, g + reach) for g in range(reach) if g + reach < groups])
        takes = jnp.logical_and(mine >= reach, mine < 2 * reach)
        reach *= 2
        if reach < groups:
            slab = jnp.where(takes, got, slab)
    if groups == 1:
        got, takes = own, mine > 0

    kept, sent = pick(pivots, me[None], prior, cores)

    if tiled:
        blocks, spots = {}, {}
        for line, (block, away) in enumerate(lines):
            at = line * near * cores
            blocks[at] = block
            for e in range(near):
                for f in range(cores):
                    spots[at + e * cores + f] = (away, e, f)
            if cores > 1:
                blocks[at + 1] = shift(block, d=1)
            if near > 1:
                blocks[at + cores] = shift(block, b=1)
                if cores > 1:
                    blocks[at + cores + 1] = shift(blocks[at + cores], d=1)
        new_block = None
        rows_of = (takes.astype(jnp.int32)[None], got)
        for number, batch in enumerate(batches(far, near, cores)):
            new_block = update(
                me[None],
                rows_of,
                old_block,
                [blocks[at] for at in batch],
                [spots[at] for at in batch],
                (far, near, cores),
                new_block,
            )
            if number == 0:
                new_block, rows_of = new_block
    else:
        every = lax.all_gather(own, "gx", axis=1, tiled=True)
        slab = jnp.where(takes, got, slab)
        new_block = old_block + jnp.dot(slab.T, every, preferred_element_type=jnp.float32)

    if cores > 1:
        kept = add(kept, shift(sent, d=1))
    if near > 1:
        kept = add(kept, shift(kept, b=1))
    bit = 1
    while bit < far:
        kept = add(kept, swap_far(kept, bit))
        bit *= 2
    picked = [kept]
    if cores > 1:
        picked.append(shift(kept, d=1))

    parts = parts_of(me[None], mine[None], prior, picked, cores, groups)
    total = parts[-1].astype(jnp.float32)
    for step in range(1, groups):
        got = lax.ppermute(parts[step - 1], "gy", [(g, (g + step) % groups) for g in range(groups)])
        total = total + got.astype(jnp.float32)
    return new_block, pair_columns - total


def batches(far, near, cores):
    if (far, near, cores) == (4, 2, 2):
        return [[0, 1, 2, 3], [4, 5, 8, 9], [6, 7, 12, 13], [10, 11, 14, 15]]
    return [list(range(at, at + near * cores)) for at in range(0, far * near * cores, near * cores)]


def solution(mesh):
    placed = (P("gx", "gy"), P(None, "gy", "gx"), P("gx", "gy"), P(("gx", "gy"), None), P())

    return jax.shard_map(
        local,
        mesh=mesh,
        in_specs=placed,
        out_specs=(P("gx", "gy"), P(("gx", "gy"), None)),
        check_vma=False,
    )
```

time: 237 us -> 105 us (0.44)
  waiting for transfers between devices: 157 us -> 38.7 us
  Pallas kernels: 0 us -> 38.3 us
  matrix products: 34.7 us -> 0 us
  starting transfers between devices: 6.59 us -> 22.7 us
  blocking collectives: 14.1 us -> 0 us
  between operations: 13.8 us -> 0.84 us
  local copies, waits for them, and re-layouts: 6.42 us -> 3.44 us
  other arithmetic: 3.57 us -> 0.87 us
    psum x2 -> x0, waiting for transfers between devices: 92.5 us -> none  [the longest x1 84.9 us: local(): pivot_block = lax.psum(chosen.astype(jnp.bfloat16), 'gx')]
    all_gather x1 -> x0, waiting for transfers between devices: 63.9 us -> none  [local(): lax.all_gather(local_vectors, 'gx', axis=1, tiled=True)]
    ppermute x0 -> x22, waiting for transfers between devices: none -> 38.7 us  [the longest x2 28 us: swap_far(): lax.ppermute(x, 'gx', [(place(i, j, k), place(i ^ bit, j, k)) for i, j, k...]
    pallas_call x0 -> x10, Pallas kernels: none -> 38.3 us  [call(): pl.pallas_call(kernel, out_shape=out_shape, in_specs=specs, out_specs=out...]
    dot_general x2 -> x0, matrix products: 34.7 us -> none  [the longest x1 29.6 us: local(): jnp.dot(slab_part.T, lax.all_gather(local_vectors, 'gx', axis=1, tiled=Tr...]
    ppermute x0 -> x22, starting transfers between devices: none -> 22.7 us  [the longest x18 17.9 us: shift(): lax.ppermute(x, 'gx', [(place(i, j, k), place(i + a, j + b, k + d)) for i...]
    all_gather x1 -> x0, blocking collectives: 14.1 us -> none  [local(): full_pivots = lax.all_gather(pivot_block, 'gy', axis=1, tiled=True)]
    all_to_all x1 -> x0, starting transfers between devices: 6.47 us -> none  [local(): lax.all_to_all(prior, 'gy', split_axis=0, concat_axis=1, tiled=True)]
  transfers between devices with their start and end apart: 4 -> 22, of which waited for: 3 -> 4; matrix products, arithmetic and copies ran while one was open for 4% -> 1% of each run, Pallas kernels for 0% -> 26%
where the time goes in v1:
time: 105 us
  waiting for transfers between devices  38.7 us (37%)
  Pallas kernels  38.3 us (36%)
  starting transfers between devices  22.7 us (22%)
  local copies, waits for them, and re-layouts  3.44 us (3%)
    pallas_call x10, Pallas kernels, call(): pl.pallas_call(kernel, out_shape=out_shape, in_specs=specs, out_specs=out...  38.3 us
    ppermute x2, waiting for transfers between devices, swap_far(): lax.ppermute(x, 'gx', [(place(i, j, k), place(i ^ bit, j, k)) for i, j, k...  28 us
    ppermute x18, starting transfers between devices, shift(): lax.ppermute(x, 'gx', [(place(i, j, k), place(i + a, j + b, k + d)) for i...  17.9 us
    ppermute x18, waiting for transfers between devices, shift(): lax.ppermute(x, 'gx', [(place(i, j, k), place(i + a, j + b, k + d)) for i...  10.7 us
    unnamed x6, local copies, waits for them, and re-layouts  3.44 us
    ppermute x1, starting transfers between devices, local(): lax.ppermute(slab, 'gy', [(g, g + reach) for g in range(reach) if g + rea...  3.41 us
  transfers between devices with their start and end apart: 22, of which 4 were waited for; matrix products, arithmetic and copies ran while one was open for 1% of the time, Pallas kernels for 26%

profile of v1, /device:TPU:0, one launch (start us, length us, event | category | flops | bytes accessed | tf_op | source)
XLA Modules:
  0.0 104.8 jit_solution(13248234593462817817)
XLA Ops:
  0.6 0.0 copy-start.1
  0.6 0.6 copy-done.1
  1.3 2.2 %shard_map.72 = (bf16[64,1536]{1,0:T(8,128)(2,1)S(1)}, bf16[64,1536]{1,0:T(8,128)(2,1)S(1)}) custom-call(s32[128]{0:T(128)S(1)} %copy-done.1, s32[1]{0:T(128)} %bitcast.me, bf16[2048,1536]{1,0:T(8,128)(2,1)} %rest_0_.1), custom_call_target="tpu_custom_call" | custom-call | tf_op jit(solution)/shard_map/pallas_call | solution.py:27
  3.5 0.7 collective-permute-start.16
  4.2 2.3 %collective-permute-start.2 = (bf16[256,768]{1,0:T(8,128)(2,1)}, bf16[256,768]{1,0:T(8,128)(2,1)S(1)}, u32[]{:S(2)}, u32[]{:S(2)}) collective-permute-start(bf16[256,768]{1,0:T(8,128)(2,1)} %bitcast.4), channel_id=1, source_target_pairs={{0,4},{2,6},{4,0},{6,2},{8,12},{10,14},{12,8},{14,10},{16,20},{18,... | collective-permute-start | bytes 1179656 | tf_op jit(solution)/shard_map/ppermute | solution.py:244
  6.4 0.0 collective-permute-done.16.b
  6.5 1.4 %collective-permute-start.17 = (bf16[64,1536]{1,0:T(8,128)(2,1)S(1)}, bf16[64,1536]{1,0:T(8,128)(2,1)S(1)}, u32[]{:S(2)}, u32[]{:S(2)}) collective-permute-start(bf16[64,1536]{1,0:T(8,128)(2,1)S(1)} %shard_map.73.a), channel_id=1, source_target_pairs={{0,4},{2,6},{4,0},{6,2},{8,12},{10,14},{12,8},{14,10},{16,20},{18,... | collective-permute-start | bytes 589832 | tf_op jit(solution)/shard_map/ppermute | solution.py:244
  7.9 3.4 %collective-permute-start = (bf16[256,768]{1,0:T(8,128)(2,1)}, bf16[256,768]{1,0:T(8,128)(2,1)S(1)}, u32[]{:S(2)}, u32[]{:S(2)}) collective-permute-start(bf16[256,768]{1,0:T(8,128)(2,1)} %bitcast.5), channel_id=1, source_target_pairs={{0,1},{2,3},{4,5},{6,7},{8,9},{10,11},{12,13},{14,15},{16,17},{18,... | collective-permute-start | bytes 1179656 | tf_op jit(solution)/shard_map/ppermute | solution.py:266
  11.3 1.7 %collective-permute-start.7 = (bf16[256,768]{1,0:T(8,128)(2,1)}, bf16[256,768]{1,0:T(8,128)(2,1)S(1)}, u32[]{:S(2)}, u32[]{:S(2)}) collective-permute-start(bf16[256,768]{1,0:T(8,128)(2,1)} %bitcast.6), channel_id=1, source_target_pairs={{0,8},{2,10},{4,12},{6,14},{8,16},{10,18},{12,20},{14,22},{16,24},... | collective-permute-start | bytes 1179656 | tf_op jit(solution)/shard_map/ppermute | solution.py:244
  13.0 0.0 collective-permute-start.1
  13.0 7.5 %collective-permute-done.17.b = bf16[64,1536]{1,0:T(8,128)(2,1)S(1)} collective-permute-done((bf16[64,1536]{1,0:T(8,128)(2,1)S(1)}, bf16[64,1536]{1,0:T(8,128)(2,1)S(1)}, u32[]{:S(2)}, u32[]{:S(2)}) %collective-permute-start.17) | collective-permute-done | bytes 196640 | tf_op jit(solution)/shard_map/ppermute | solution.py:244
  20.6 4.1 %collective-permute-start.4 = (bf16[256,768]{1,0:T(8,128)(2,1)}, bf16[256,768]{1,0:T(8,128)(2,1)S(1)}, u32[]{:S(2)}, u32[]{:S(2)}) collective-permute-start(bf16[256,768]{1,0:T(8,128)(2,1)} %bitcast.8), channel_id=1, source_target_pairs={{0,24},{2,26},{4,28},{6,30},{8,0},{10,2},{12,4},{14,6},{16,8},{18,... | collective-permute-start | bytes 1179656 | tf_op jit(solution)/shard_map/ppermute | solution.py:244
  24.7 0.0 collective-permute-done.2.rest_4_
  24.7 0.1 collective-permute-start.18
  24.8 0.0 collective-permute-done.rest_2_
  24.8 0.1 collective-permute-start.3
  24.9 0.0 collective-permute-done.7.rest_1_
  24.9 0.5 collective-permute-start.14
  25.4 11.8 %collective-permute-done.18.b = bf16[64,1536]{1,0:T(8,128)(2,1)S(1)} collective-permute-done((bf16[64,1536]{1,0:T(8,128)(2,1)S(1)}, bf16[64,1536]{1,0:T(8,128)(2,1)S(1)}, u32[]{:S(2)}, u32[]{:S(2)}) %collective-permute-start.18) | collective-permute-done | bytes 196640 | tf_op jit(solution)/shard_map/ppermute | solution.py:247
  37.2 2.5 %collective-permute-start.8 = (bf16[256,768]{1,0:T(8,128)(2,1)S(1)}, bf16[256,768]{1,0:T(8,128)(2,1)S(1)}, u32[]{:S(2)}, u32[]{:S(2)}) collective-permute-start(bf16[256,768]{1,0:T(8,128)(2,1)S(1)} %collective-permute-done.7.rest_1_), channel_id=1, source_target_pairs={{0,8},{2,10},{4,12},{6,14},{8,16},{10,18},{12,20},{14,22},{16,24},... | collective-permute-start | bytes 1179656 | tf_op jit(solution)/shard_map/ppermute | solution.py:244
  39.7 0.0 collective-permute-done.1.rest_3_
  39.7 0.5 collective-permute-start.19
  40.3 0.0 collective-permute-done.4.rest_3_
  40.3 1.5 %collective-permute-start.11 = (bf16[256,768]{1,0:T(8,128)(2,1)S(1)}, bf16[256,768]{1,0:T(8,128)(2,1)}, u32[]{:S(2)}, u32[]{:S(2)}) collective-permute-start(bf16[256,768]{1,0:T(8,128)(2,1)S(1)} %collective-permute-done.7.rest_1_), channel_id=1, source_target_pairs={{0,4},{2,6},{4,0},{6,2},{8,12},{10,14},{12,8},{14,10},{16,20},{18,... | collective-permute-start | bytes 1179656 | tf_op jit(solution)/shard_map/ppermute | solution.py:244
  41.8 16.2 %collective-permute-done.19.b = bf16[64,1536]{1,0:T(8,128)(2,1)S(1)} collective-permute-done((bf16[64,1536]{1,0:T(8,128)(2,1)S(1)}, bf16[64,1536]{1,0:T(8,128)(2,1)S(1)}, u32[]{:S(2)}, u32[]{:S(2)}) %collective-permute-start.19) | collective-permute-done | bytes 196640 | tf_op jit(solution)/shard_map/ppermute | solution.py:247
  58.0 0.0 collective-permute-start.15
  58.0 0.0 collective-permute-done.3.rest_5_
  58.1 0.6 collective-permute-start.20
  58.6 0.0 collective-permute-done.14.rest_2_
  58.6 0.6 collective-permute-start.5
  59.2 0.0 collective-permute-done.8.rest_3_
  59.2 1.4 %collective-permute-start.9 = (bf16[256,768]{1,0:T(8,128)(2,1)S(1)}, bf16[256,768]{1,0:T(8,128)(2,1)}, u32[]{:S(2)}, u32[]{:S(2)}) collective-permute-start(bf16[256,768]{1,0:T(8,128)(2,1)S(1)} %collective-permute-done.8.rest_3_), channel_id=1, source_target_pairs={{0,4},{2,6},{4,0},{6,2},{8,12},{10,14},{12,8},{14,10},{16,20},{18,... | collective-permute-start | bytes 1179656 | tf_op jit(solution)/shard_map/ppermute | solution.py:244
  60.6 0.0 collective-permute-done.11.rest_1_
  60.6 0.0 collective-permute-start.13
  60.7 0.0 collective-permute-done.20.rest_2_
  60.7 0.5 collective-permute-start.12
  61.2 0.0 copy-start
  61.2 2.8 %copy-done = bf16[2048,1536]{1,0:T(8,128)(2,1)S(1)} copy-done((bf16[2048,1536]{1,0:T(8,128)(2,1)S(1)}, bf16[2048,1536]{1,0:T(8,128)(2,1)}, u32[]{:S(2)}) %copy-start) | copy-done | bytes 6291480
  64.0 1.8 %shard_map.77 = (bf16[1024,128]{1,0:T(8,128)(2,1)S(1)}, bf16[1024,128]{1,0:T(8,128)(2,1)S(1)}) custom-call(s32[1]{0:T(128)} %bitcast.me, s32[1]{0:T(128)} %bitcast.3.mine, bf16[2048,1536]{1,0:T(8,128)(2,1)S(1)} %copy-done, bf16[64,1536]{1,0:T(8,128)(2,1)S(1)} %shard_map.76.rest_1_, bf16[64,1536]{1,0:T(8,128)(2,1)S(1)} %collective-permute-done.20.rest_2_), custom_call_target="tpu_custom_call" | custom-call | tf_op jit(solution)/shard_map/pallas_call | solution.py:27
  65.7 0.0 collective-permute-done.15.rest_4_
  65.8 0.7 collective-permute-start.21
  66.5 8.6 %shard_map.68 = (f32[768,12288]{1,0:T(8,128)}, bf16[768,256]{1,0:T(8,128)(2,1)S(1)}) custom-call(s32[1]{0:T(128)} %bitcast.me, s32[1]{0:T(128)} %bitcast.1.rest_0_, bf16[256,768]{1,0:T(8,128)(2,1)} %bitcast.9, bf16[256,768]{1,0:T(8,128)(2,1)S(1)} %collective-permute-done.rest_2_, bf16[256,768]{1,0:T(8,128)(2,1)S(1)} %collective-permute-done.1.rest_3_, ...), custom_call_target="tpu_custom_call" | custom-call | flops 1207959552 | tf_op jit(solution)/shard_map/pallas_call | solution.py:27
  75.1 0.0 collective-permute-done.5.rest_1_
  75.1 0.1 collective-permute-start.6
  75.2 3.1 %collective-permute-done.9.rest_3_ = bf16[256,768]{1,0:T(8,128)(2,1)} collective-permute-done((bf16[256,768]{1,0:T(8,128)(2,1)S(1)}, bf16[256,768]{1,0:T(8,128)(2,1)}, u32[]{:S(2)}, u32[]{:S(2)}) %collective-permute-start.9) | collective-permute-done | bytes 393248 | tf_op jit(solution)/shard_map/ppermute | solution.py:244
  78.3 0.0 collective-permute-start.10
  78.3 8.4 %shard_map.69.rest_6_ = f32[768,12288]{1,0:T(8,128)} custom-call(s32[1]{0:T(128)} %bitcast.me, bf16[768,256]{1,0:T(8,128)(2,1)S(1)} %get-tuple-element.8.rest_0_, bf16[256,768]{1,0:T(8,128)(2,1)S(1)} %collective-permute-done.7.rest_1_, bf16[256,768]{1,0:T(8,128)(2,1)S(1)} %collective-permute-done.14.rest_2_, ...), custom_call_target="tpu_custom_call", output_to_operand_aliasing={{}: (7, {})} | custom-call | flops 1207959552 | tf_op jit(solution)/shard_map/pallas_call | solution.py:27
  86.7 0.0 copy-start.2
  86.7 0.0 collective-permute-done.13.rest_4_
  86.7 0.0 collective-permute-done.12.rest_2_
  86.7 8.7 %shard_map.70.rest_6_ = f32[768,12288]{1,0:T(8,128)} custom-call(s32[1]{0:T(128)} %bitcast.me, bf16[768,256]{1,0:T(8,128)(2,1)S(1)} %get-tuple-element.8.rest_0_, bf16[256,768]{1,0:T(8,128)(2,1)} %collective-permute-done.11.rest_1_, bf16[256,768]{1,0:T(8,128)(2,1)} %collective-permute-done.12.rest_2_, ...), custom_call_target="tpu_custom_call", output_to_operand_aliasing={{}: (7, {})} | custom-call | flops 1207959552 | tf_op jit(solution)/shard_map/pallas_call | solution.py:27
  95.4 0.0 collective-permute-done.21
  95.4 0.0 copy-done.2
  95.4 0.9 add_subtract_fusion
  96.3 0.0 collective-permute-done.6.rest_2_
  96.3 0.0 collective-permute-done.10.rest_4_
  96.3 8.5 %shard_map.71 = f32[768,12288]{1,0:T(8,128)} custom-call(s32[1]{0:T(128)} %bitcast.me, bf16[768,256]{1,0:T(8,128)(2,1)S(1)} %get-tuple-element.8.rest_0_, bf16[256,768]{1,0:T(8,128)(2,1)} %collective-permute-done.5.rest_1_, bf16[256,768]{1,0:T(8,128)(2,1)S(1)} %collective-permute-done.6.rest_2_, ...), custom_call_target="tpu_custom_call", output_to_operand_aliasing={{}: (7, {})} | custom-call | flops 1207959552 | tf_op jit(solution)/shard_map/pallas_call | solution.py:27
  (4 shorter events, 0.1 us)
Async XLA Ops:
  0.6 0.7 copy-start.1
  3.5 2.9 %collective-permute-start.16 = (bf16[64,1536]{1,0:T(8,128)(2,1)S(1)}, bf16[64,1536]{1,0:T(8,128)(2,1)S(1)}, u32[]{:S(2)}, u32[]{:S(2)}) collective-permute-start(bf16[64,1536]{1,0:T(8,128)(2,1)S(1)} %get-tuple-element.11), channel_id=1, source_target_pairs={{0,2},{2,0},{4,6},{6,4},{8,10},{10,8},{12,14},{14,12},{16,18},{18,... | collective-permute-start | bytes 589832 | tf_op jit(solution)/shard_map/ppermute | solution.py:244
  4.2 20.5 %collective-permute-start.2 = (bf16[256,768]{1,0:T(8,128)(2,1)}, bf16[256,768]{1,0:T(8,128)(2,1)S(1)}, u32[]{:S(2)}, u32[]{:S(2)}) collective-permute-start(bf16[256,768]{1,0:T(8,128)(2,1)} %bitcast.4), channel_id=1, source_target_pairs={{0,4},{2,6},{4,0},{6,2},{8,12},{10,14},{12,8},{14,10},{16,20},{18,... | collective-permute-start | bytes 1179656 | tf_op jit(solution)/shard_map/ppermute | solution.py:244
  6.5 14.1 %collective-permute-start.17 = (bf16[64,1536]{1,0:T(8,128)(2,1)S(1)}, bf16[64,1536]{1,0:T(8,128)(2,1)S(1)}, u32[]{:S(2)}, u32[]{:S(2)}) collective-permute-start(bf16[64,1536]{1,0:T(8,128)(2,1)S(1)} %shard_map.73.a), channel_id=1, source_target_pairs={{0,4},{2,6},{4,0},{6,2},{8,12},{10,14},{12,8},{14,10},{16,20},{18,... | collective-permute-start | bytes 589832 | tf_op jit(solution)/shard_map/ppermute | solution.py:244
  7.9 16.9 %collective-permute-start = (bf16[256,768]{1,0:T(8,128)(2,1)}, bf16[256,768]{1,0:T(8,128)(2,1)S(1)}, u32[]{:S(2)}, u32[]{:S(2)}) collective-permute-start(bf16[256,768]{1,0:T(8,128)(2,1)} %bitcast.5), channel_id=1, source_target_pairs={{0,1},{2,3},{4,5},{6,7},{8,9},{10,11},{12,13},{14,15},{16,17},{18,... | collective-permute-start | bytes 1179656 | tf_op jit(solution)/shard_map/ppermute | solution.py:266
  11.3 13.6 %collective-permute-start.7 = (bf16[256,768]{1,0:T(8,128)(2,1)}, bf16[256,768]{1,0:T(8,128)(2,1)S(1)}, u32[]{:S(2)}, u32[]{:S(2)}) collective-permute-start(bf16[256,768]{1,0:T(8,128)(2,1)} %bitcast.6), channel_id=1, source_target_pairs={{0,8},{2,10},{4,12},{6,14},{8,16},{10,18},{12,20},{14,22},{16,24},... | collective-permute-start | bytes 1179656 | tf_op jit(solution)/shard_map/ppermute | solution.py:244
  13.0 26.7 %collective-permute-start.1 = (bf16[256,768]{1,0:T(8,128)(2,1)}, bf16[256,768]{1,0:T(8,128)(2,1)S(1)}, u32[]{:S(2)}, u32[]{:S(2)}) collective-permute-start(bf16[256,768]{1,0:T(8,128)(2,1)} %bitcast.7), channel_id=1, source_target_pairs={{0,2},{2,0},{4,6},{6,4},{8,10},{10,8},{12,14},{14,12},{16,18},{18,... | collective-permute-start | bytes 1179656 | tf_op jit(solution)/shard_map/ppermute | solution.py:244
  20.6 19.7 %collective-permute-start.4 = (bf16[256,768]{1,0:T(8,128)(2,1)}, bf16[256,768]{1,0:T(8,128)(2,1)S(1)}, u32[]{:S(2)}, u32[]{:S(2)}) collective-permute-start(bf16[256,768]{1,0:T(8,128)(2,1)} %bitcast.8), channel_id=1, source_target_pairs={{0,24},{2,26},{4,28},{6,30},{8,0},{10,2},{12,4},{14,6},{16,8},{18,... | collective-permute-start | bytes 1179656 | tf_op jit(solution)/shard_map/ppermute | solution.py:244
  24.7 12.5 %collective-permute-start.18 = (bf16[64,1536]{1,0:T(8,128)(2,1)S(1)}, bf16[64,1536]{1,0:T(8,128)(2,1)S(1)}, u32[]{:S(2)}, u32[]{:S(2)}) collective-permute-start(bf16[64,1536]{1,0:T(8,128)(2,1)S(1)} %shard_map.74.a), channel_id=1, source_target_pairs={{0,8},{2,10},{4,12},{6,14},{8,0},{10,2},{12,4},{14,6},{16,24},{18,... | collective-permute-start | bytes 589832 | tf_op jit(solution)/shard_map/ppermute | solution.py:247
  24.8 33.2 %collective-permute-start.3 = (bf16[256,768]{1,0:T(8,128)(2,1)S(1)}, bf16[256,768]{1,0:T(8,128)(2,1)S(1)}, u32[]{:S(2)}, u32[]{:S(2)}) collective-permute-start(bf16[256,768]{1,0:T(8,128)(2,1)S(1)} %collective-permute-done.2.rest_4_), channel_id=1, source_target_pairs={{0,2},{2,0},{4,6},{6,4},{8,10},{10,8},{12,14},{14,12},{16,18},{18,... | collective-permute-start | bytes 1179656 | tf_op jit(solution)/shard_map/ppermute | solution.py:244
  24.9 33.7 %collective-permute-start.14 = (bf16[256,768]{1,0:T(8,128)(2,1)S(1)}, bf16[256,768]{1,0:T(8,128)(2,1)S(1)}, u32[]{:S(2)}, u32[]{:S(2)}) collective-permute-start(bf16[256,768]{1,0:T(8,128)(2,1)S(1)} %collective-permute-done.7.rest_1_), channel_id=1, source_target_pairs={{0,2},{2,0},{4,6},{6,4},{8,10},{10,8},{12,14},{14,12},{16,18},{18,... | collective-permute-start | bytes 1179656 | tf_op jit(solution)/shard_map/ppermute | solution.py:244
  37.2 22.0 %collective-permute-start.8 = (bf16[256,768]{1,0:T(8,128)(2,1)S(1)}, bf16[256,768]{1,0:T(8,128)(2,1)S(1)}, u32[]{:S(2)}, u32[]{:S(2)}) collective-permute-start(bf16[256,768]{1,0:T(8,128)(2,1)S(1)} %collective-permute-done.7.rest_1_), channel_id=1, source_target_pairs={{0,8},{2,10},{4,12},{6,14},{8,16},{10,18},{12,20},{14,22},{16,24},... | collective-permute-start | bytes 1179656 | tf_op jit(solution)/shard_map/ppermute | solution.py:244
  39.7 18.3 %collective-permute-start.19 = (bf16[64,1536]{1,0:T(8,128)(2,1)S(1)}, bf16[64,1536]{1,0:T(8,128)(2,1)S(1)}, u32[]{:S(2)}, u32[]{:S(2)}) collective-permute-start(bf16[64,1536]{1,0:T(8,128)(2,1)S(1)} %shard_map.75.a), channel_id=1, source_target_pairs={{0,16},{2,18},{4,20},{6,22},{8,24},{10,26},{12,28},{14,30},{16,0},... | collective-permute-start | bytes 589832 | tf_op jit(solution)/shard_map/ppermute | solution.py:247
  40.3 20.4 %collective-permute-start.11 = (bf16[256,768]{1,0:T(8,128)(2,1)S(1)}, bf16[256,768]{1,0:T(8,128)(2,1)}, u32[]{:S(2)}, u32[]{:S(2)}) collective-permute-start(bf16[256,768]{1,0:T(8,128)(2,1)S(1)} %collective-permute-done.7.rest_1_), channel_id=1, source_target_pairs={{0,4},{2,6},{4,0},{6,2},{8,12},{10,14},{12,8},{14,10},{16,20},{18,... | collective-permute-start | bytes 1179656 | tf_op jit(solution)/shard_map/ppermute | solution.py:244
  58.0 7.8 %collective-permute-start.15 = (bf16[256,768]{1,0:T(8,128)(2,1)S(1)}, bf16[256,768]{1,0:T(8,128)(2,1)}, u32[]{:S(2)}, u32[]{:S(2)}) collective-permute-start(bf16[256,768]{1,0:T(8,128)(2,1)S(1)} %collective-permute-done.4.rest_3_), channel_id=1, source_target_pairs={{0,2},{2,0},{4,6},{6,4},{8,10},{10,8},{12,14},{14,12},{16,18},{18,... | collective-permute-start | bytes 1179656 | tf_op jit(solution)/shard_map/ppermute | solution.py:244
  58.1 2.6 %collective-permute-start.20 = (bf16[64,1536]{1,0:T(8,128)(2,1)S(1)}, bf16[64,1536]{1,0:T(8,128)(2,1)S(1)}, u32[]{:S(2)}, u32[]{:S(2)}) collective-permute-start(bf16[64,1536]{1,0:T(8,128)(2,1)S(1)} %shard_map.76.rest_1_), channel_id=1, source_target_pairs={{0,2},{2,0},{4,6},{6,4},{8,10},{10,8},{12,14},{14,12},{16,18},{18,... | collective-permute-start | bytes 589832 | tf_op jit(solution)/shard_map/ppermute | solution.py:244
  58.6 16.5 %collective-permute-start.5 = (bf16[256,768]{1,0:T(8,128)(2,1)S(1)}, bf16[256,768]{1,0:T(8,128)(2,1)}, u32[]{:S(2)}, u32[]{:S(2)}) collective-permute-start(bf16[256,768]{1,0:T(8,128)(2,1)S(1)} %collective-permute-done.4.rest_3_), channel_id=1, source_target_pairs={{0,4},{2,6},{4,0},{6,2},{8,12},{10,14},{12,8},{14,10},{16,20},{18,... | collective-permute-start | bytes 1179656 | tf_op jit(solution)/shard_map/ppermute | solution.py:244
  59.2 19.0 %collective-permute-start.9 = (bf16[256,768]{1,0:T(8,128)(2,1)S(1)}, bf16[256,768]{1,0:T(8,128)(2,1)}, u32[]{:S(2)}, u32[]{:S(2)}) collective-permute-start(bf16[256,768]{1,0:T(8,128)(2,1)S(1)} %collective-permute-done.8.rest_3_), channel_id=1, source_target_pairs={{0,4},{2,6},{4,0},{6,2},{8,12},{10,14},{12,8},{14,10},{16,20},{18,... | collective-permute-start | bytes 1179656 | tf_op jit(solution)/shard_map/ppermute | solution.py:244
  60.6 26.0 %collective-permute-start.13 = (bf16[256,768]{1,0:T(8,128)(2,1)S(1)}, bf16[256,768]{1,0:T(8,128)(2,1)}, u32[]{:S(2)}, u32[]{:S(2)}) collective-permute-start(bf16[256,768]{1,0:T(8,128)(2,1)S(1)} %collective-permute-done.8.rest_3_), channel_id=1, source_target_pairs={{0,2},{2,0},{4,6},{6,4},{8,10},{10,8},{12,14},{14,12},{16,18},{18,... | collective-permute-start | bytes 1179656 | tf_op jit(solution)/shard_map/ppermute | solution.py:244
  60.7 26.0 %collective-permute-start.12 = (bf16[256,768]{1,0:T(8,128)(2,1)}, bf16[256,768]{1,0:T(8,128)(2,1)}, u32[]{:S(2)}, u32[]{:S(2)}) collective-permute-start(bf16[256,768]{1,0:T(8,128)(2,1)} %collective-permute-done.11.rest_1_), channel_id=1, source_target_pairs={{0,2},{2,0},{4,6},{6,4},{8,10},{10,8},{12,14},{14,12},{16,18},{18,... | collective-permute-start | bytes 1179656 | tf_op jit(solution)/shard_map/ppermute | solution.py:244
  61.2 2.8 %copy-start = (bf16[2048,1536]{1,0:T(8,128)(2,1)S(1)}, bf16[2048,1536]{1,0:T(8,128)(2,1)}, u32[]{:S(2)}) copy-start(bf16[2048,1536]{1,0:T(8,128)(2,1)} %rest_0_.1) | copy-start | bytes 18874372
  65.8 29.6 %collective-permute-start.21 = (bf16[1024,128]{1,0:T(8,128)(2,1)S(1)}, bf16[1024,128]{1,0:T(8,128)(2,1)S(1)}, u32[]{:S(2)}, u32[]{:S(2)}) collective-permute-start(bf16[1024,128]{1,0:T(8,128)(2,1)S(1)} %get-tuple-element.13), channel_id=1, source_target_pairs={{0,1},{1,0},{2,3},{3,2},{4,5},{5,4},{6,7},{7,6},{8,9},{9,8},{10,11... | collective-permute-start | bytes 786440 | tf_op jit(solution)/shard_map/ppermute | solution.py:324
  75.1 21.2 %collective-permute-start.6 = (bf16[256,768]{1,0:T(8,128)(2,1)}, bf16[256,768]{1,0:T(8,128)(2,1)S(1)}, u32[]{:S(2)}, u32[]{:S(2)}) collective-permute-start(bf16[256,768]{1,0:T(8,128)(2,1)} %collective-permute-done.5.rest_1_), channel_id=1, source_target_pairs={{0,2},{2,0},{4,6},{6,4},{8,10},{10,8},{12,14},{14,12},{16,18},{18,... | collective-permute-start | bytes 1179656 | tf_op jit(solution)/shard_map/ppermute | solution.py:244
  78.3 18.1 %collective-permute-start.10 = (bf16[256,768]{1,0:T(8,128)(2,1)}, bf16[256,768]{1,0:T(8,128)(2,1)S(1)}, u32[]{:S(2)}, u32[]{:S(2)}) collective-permute-start(bf16[256,768]{1,0:T(8,128)(2,1)} %collective-permute-done.9.rest_3_), channel_id=1, source_target_pairs={{0,2},{2,0},{4,6},{6,4},{8,10},{10,8},{12,14},{14,12},{16,18},{18,... | collective-permute-start | bytes 1179656 | tf_op jit(solution)/shard_map/ppermute | solution.py:244
  86.7 8.7 %copy-start.2 = (f32[1024,128]{1,0:T(8,128)S(1)}, f32[1024,128]{1,0:T(8,128)}, u32[]{:S(2)}) copy-start(f32[1024,128]{1,0:T(8,128)} %param.8) | copy-start | bytes 1572868

commit v2 on v1

--- a/solution.py
+++ b/solution.py
@@ -36,20 +36,25 @@
     )(*operands)
 
 
-def update_kernel(me, *rest, spots, extent, tiles, first):
+def update_kernel(me, *rest, spots, extent, tiles, first, tail):
     far, near, cores = extent
     count = len(spots)
+    if tail:
+        rest, (total, pair_in, pair_out) = rest[:-3], rest[-3:]
     held, arrive, leave = rest[-3:]
     high, width = held.shape[1:]
     z, y, c = me[0] // (near * cores), me[0] // cores % near, me[0] % cores
     pieces = [(at, tile) for at in range(count) for tile in range(tiles)]
+    lag = 3 if len(pieces) >= 8 else 0
     if first:
         mask, own, got, *blocks = rest[: count + 2]
         old, out, slab, mine, here = rest[count + 2 : count + 7]
         blocks = [mine, *blocks]
     else:
         slab, *blocks = rest[: count + 1]
-        old, out = rest[count + 1], rest[-4]
+        old = rest[count + 1]
+        pair, *parts = rest[count + 3 : count + 3 + tail] if tail else [None]
+        out = rest[count + 3 + tail]
 
     def spot(at, tile):
         a, b, d = spots[at]
@@ -67,6 +72,11 @@
         bring.start()
     for n in range(len(pieces)):
         load(n).start()
+    if tail:
+        residual = rest[count + 4 + tail]
+        pair_load = pltpu.make_async_copy(pair, total, pair_in)
+        pair_save = pltpu.make_async_copy(total, residual, pair_out)
+        pair_load.start()
     if first:
         bring.wait()
         chosen = jnp.where(mask[0] != 0, got[...].astype(jnp.float32), mine[...].astype(jnp.float32))
@@ -76,17 +86,29 @@
         held[n] += jnp.dot(
             slab[tile * high : (tile + 1) * high, :], blocks[at][...], preferred_element_type=jnp.float32
         )
+        if n >= lag:
+            save(n - lag).start()
+    if tail:
+        pair_load.wait()
+        gathered = parts[0][...].astype(jnp.float32)
+        for part in parts[1:]:
+            gathered = gathered + part[...].astype(jnp.float32)
+        total[...] -= gathered
+        pair_save.start()
+    for n in range(len(pieces) - lag, len(pieces)):
         save(n).start()
+    if tail:
+        pair_save.wait()
     for n in range(len(pieces)):
         save(n).wait()
 
 
-def update(me, rows_of, old, blocks, spots, extent, target):
+def update(me, rows_of, old, blocks, spots, extent, target, tail=()):
     first = target is None
     inner, width = blocks[-1].shape
     rows = old.shape[0]
     count = len(blocks)
-    tiles = next(t for t in (3, 2, 1) if rows % (8 * t) == 0)
+    tiles = next(t for t in (2, 1) if rows % (8 * t) == 0)
     high = rows // tiles
     shape = jax.ShapeDtypeStruct(old.shape, old.dtype)
     scratch = [
@@ -106,9 +128,19 @@
         operands = [me, rows_of, *blocks, keep(old), target]
         specs = [SMEM, VMEM] + [VMEM] * count + [HBM, HBM]
         aliases = {len(operands) - 1: 0}
-        outs, out_specs = shape, HBM
+        outs, out_specs = [shape], [HBM]
+        if tail:
+            operands += [keep(tail[0]), *tail[1:]]
+            specs += [HBM] + [VMEM] * (len(tail) - 1)
+            outs.append(jax.ShapeDtypeStruct(tail[0].shape, tail[0].dtype))
+            out_specs.append(HBM)
+            scratch += [
+                pltpu.VMEM(tail[0].shape, tail[0].dtype),
+                pltpu.SemaphoreType.DMA,
+                pltpu.SemaphoreType.DMA,
+            ]
     return call(
-        functools.partial(update_kernel, spots=spots, extent=extent, tiles=tiles, first=first),
+        functools.partial(update_kernel, spots=spots, extent=extent, tiles=tiles, first=first, tail=len(tail)),
         outs,
         operands,
         specs,
@@ -263,13 +295,15 @@
     slab = own
     reach = 1
     while reach < groups:
-        got = lax.ppermute(slab, "gy", [(g, g + reach) for g in range(reach) if g + reach < groups])
+        got = lax.ppermute(slab, "gy", [(g, (g + reach) % groups) for g in range(groups)])
         takes = jnp.logical_and(mine >= reach, mine < 2 * reach)
         reach *= 2
         if reach < groups:
             slab = jnp.where(takes, got, slab)
     if groups == 1:
         got, takes = own, mine > 0
+    if groups > 2:
+        got, takes = jnp.where(takes, got, slab), mine >= 0
 
     kept, sent = pick(pivots, me[None], prior, cores)
 
@@ -287,24 +321,6 @@
                 blocks[at + cores] = shift(block, b=1)
                 if cores > 1:
                     blocks[at + cores + 1] = shift(blocks[at + cores], d=1)
-        new_block = None
-        rows_of = (takes.astype(jnp.int32)[None], got)
-        for number, batch in enumerate(batches(far, near, cores)):
-            new_block = update(
-                me[None],
-                rows_of,
-                old_block,
-                [blocks[at] for at in batch],
-                [spots[at] for at in batch],
-                (far, near, cores),
-                new_block,
-            )
-            if number == 0:
-                new_block, rows_of = new_block
-    else:
-        every = lax.all_gather(own, "gx", axis=1, tiled=True)
-        slab = jnp.where(takes, got, slab)
-        new_block = old_block + jnp.dot(slab.T, every, preferred_element_type=jnp.float32)
 
     if cores > 1:
         kept = add(kept, shift(sent, d=1))
@@ -319,16 +335,42 @@
         picked.append(shift(kept, d=1))
 
     parts = parts_of(me[None], mine[None], prior, picked, cores, groups)
+    arrived = []
+    for step in range(1, groups):
+        arrived.append(lax.ppermute(parts[step - 1], "gy", [(g, (g + step) % groups) for g in range(groups)]))
+
+    if tiled:
+        new_block = None
+        order = batches(far, near, cores)
+        rows_of = (takes.astype(jnp.int32)[None], got)
+        for number, batch in enumerate(order):
+            done = update(
+                me[None],
+                rows_of,
+                old_block,
+                [blocks[at] for at in batch],
+                [spots[at] for at in batch],
+                (far, near, cores),
+                new_block,
+                (pair_columns, parts[-1], *arrived) if batch == order[-1] else (),
+            )
+            new_block = done[0]
+            if number == 0:
+                rows_of = done[1]
+        return new_block, done[1]
+
+    every = lax.all_gather(own, "gx", axis=1, tiled=True)
+    slab = jnp.where(takes, got, slab)
+    new_block = old_block + jnp.dot(slab.T, every, preferred_element_type=jnp.float32)
     total = parts[-1].astype(jnp.float32)
-    for step in range(1, groups):
-        got = lax.ppermute(parts[step - 1], "gy", [(g, (g + step) % groups) for g in range(groups)])
-        total = total + got.astype(jnp.float32)
+    for part in arrived:
+        total = total + part.astype(jnp.float32)
     return new_block, pair_columns - total
 
 
 def batches(far, near, cores):
     if (far, near, cores) == (4, 2, 2):
-        return [[0, 1, 2, 3], [4, 5, 8, 9], [6, 7, 12, 13], [10, 11, 14, 15]]
+        return [[0, 1], [2, 3, 4, 5], [6, 7, 12, 13], [14, 15, 8, 9], [10, 11]]
     return [list(range(at, at + near * cores)) for at in range(0, far * near * cores, near * cores)]
 
 

time: 105 us -> 93.7 us (0.89)
  starting transfers between devices: 22.7 us -> 18 us
  waiting for transfers between devices: 38.7 us -> 35.9 us
  local copies, waits for them, and re-layouts: 3.44 us -> 1.47 us
  Pallas kernels: 38.3 us -> 37.1 us
    ppermute x2, waiting for transfers between devices: 28 us -> 19.8 us  [swap_far(): lax.ppermute(x, 'gx', [(place(i, j, k), place(i ^ bit, j, k)) for i, j, k...]
    ppermute x18, starting transfers between devices: 17.9 us -> 12 us  [shift(): lax.ppermute(x, 'gx', [(place(i, j, k), place(i + a, j + b, k + d)) for i...]
    ppermute x18, waiting for transfers between devices: 10.7 us -> 15.5 us  [shift(): lax.ppermute(x, 'gx', [(place(i, j, k), place(i + a, j + b, k + d)) for i...]
    unnamed x6 -> x18, local copies, waits for them, and re-layouts: 3.44 us -> 1.47 us
    ppermute x2, starting transfers between devices: 0.59 us -> 2.32 us  [swap_far(): lax.ppermute(x, 'gx', [(place(i, j, k), place(i ^ bit, j, k)) for i, j, k...]
    pallas_call x10 -> x11, Pallas kernels: 38.3 us -> 37.1 us  [call(): pl.pallas_call(kernel, out_shape=out_shape, in_specs=specs, out_specs=out...]
  transfers between devices with their start and end apart: 22 -> 22, of which waited for: 4 -> 6; matrix products, arithmetic and copies ran while one was open for 1% -> 0% of each run, Pallas kernels for 26% -> 35%
where the time goes in v2:
time: 93.7 us; the launch traced here: 93.3 us
  Pallas kernels  37.1 us (40%)
  waiting for transfers between devices  35.9 us (38%)
  starting transfers between devices  18 us (19%)
  local copies, waits for them, and re-layouts  1.47 us (2%)
    pallas_call x11, Pallas kernels, call(): pl.pallas_call(kernel, out_shape=out_shape, in_specs=specs, out_specs=out...  37.1 us
    ppermute x2, waiting for transfers between devices, swap_far(): lax.ppermute(x, 'gx', [(place(i, j, k), place(i ^ bit, j, k)) for i, j, k...  19.8 us
    ppermute x18, waiting for transfers between devices, shift(): lax.ppermute(x, 'gx', [(place(i, j, k), place(i + a, j + b, k + d)) for i...  15.5 us
    ppermute x18, starting transfers between devices, shift(): lax.ppermute(x, 'gx', [(place(i, j, k), place(i + a, j + b, k + d)) for i...  12 us
    ppermute x1, starting transfers between devices, local(): lax.ppermute(slab, 'gy', [(g, (g + reach) % groups) for g in range(groups)])  3.03 us
    ppermute x2, starting transfers between devices, swap_far(): lax.ppermute(x, 'gx', [(place(i, j, k), place(i ^ bit, j, k)) for i, j, k...  2.32 us
  transfers between devices with their start and end apart: 22, of which 6 were waited for; matrix products, arithmetic and copies ran while one was open for 0% of the time, Pallas kernels for 35%

profile of v2, /device:TPU:0, one launch (start us, length us, event | category | flops | bytes accessed | tf_op | source)
XLA Modules:
  0.0 93.3 jit_solution(8543157431132995763)
XLA Ops:
  0.6 0.0 slice-start
  0.6 3.0 %collective-permute-start = (bf16[256,768]{1,0:T(8,128)(2,1)}, bf16[256,768]{1,0:T(8,128)(2,1)S(1)}, u32[]{:S(2)}, u32[]{:S(2)}) collective-permute-start(bf16[256,768]{1,0:T(8,128)(2,1)} %bitcast.6), channel_id=1, source_target_pairs={{0,1},{1,0},{2,3},{3,2},{4,5},{5,4},{6,7},{7,6},{8,9},{9,8},{10,11... | collective-permute-start | bytes 1179656 | tf_op jit(solution)/shard_map/ppermute | solution.py:298
  3.7 1.6 %collective-permute-start.5 = (bf16[256,768]{1,0:T(8,128)(2,1)}, bf16[256,768]{1,0:T(8,128)(2,1)}, u32[]{:S(2)}, u32[]{:S(2)}) collective-permute-start(bf16[256,768]{1,0:T(8,128)(2,1)} %bitcast.7), channel_id=1, source_target_pairs={{0,8},{2,10},{4,12},{6,14},{8,16},{10,18},{12,20},{14,22},{16,24},... | collective-permute-start | bytes 1179656 | tf_op jit(solution)/shard_map/ppermute | solution.py:276
  5.3 0.0 collective-permute-start.1
  5.3 0.7 copy-done.6
  5.9 2.2 %shard_map.72 = (bf16[64,1536]{1,0:T(8,128)(2,1)S(1)}, bf16[64,1536]{1,0:T(8,128)(2,1)S(1)}) custom-call(s32[128]{0:T(128)S(1)} %copy-done.6, s32[1]{0:T(128)} %bitcast.me, bf16[2048,1536]{1,0:T(8,128)(2,1)} %rest_0_.1), custom_call_target="tpu_custom_call" | custom-call | tf_op jit(solution)/shard_map/pallas_call | solution.py:27
  8.2 0.7 collective-permute-start.16
  8.8 1.3 %collective-permute-start.13 = (bf16[256,768]{1,0:T(8,128)(2,1)}, bf16[256,768]{1,0:T(8,128)(2,1)S(1)}, u32[]{:S(2)}, u32[]{:S(2)}) collective-permute-start(bf16[256,768]{1,0:T(8,128)(2,1)} %bitcast.9), channel_id=1, source_target_pairs={{0,4},{2,6},{4,0},{6,2},{8,12},{10,14},{12,8},{14,10},{16,20},{18,... | collective-permute-start | bytes 1179656 | tf_op jit(solution)/shard_map/ppermute | solution.py:276
  10.1 0.0 collective-permute-done.16.b
  10.1 2.2 %collective-permute-start.2 = (bf16[256,768]{1,0:T(8,128)(2,1)}, bf16[256,768]{1,0:T(8,128)(2,1)}, u32[]{:S(2)}, u32[]{:S(2)}) collective-permute-start(bf16[256,768]{1,0:T(8,128)(2,1)} %bitcast.10), channel_id=1, source_target_pairs={{0,24},{2,26},{4,28},{6,30},{8,0},{10,2},{12,4},{14,6},{16,8},{18,... | collective-permute-start | bytes 1179656 | tf_op jit(solution)/shard_map/ppermute | solution.py:276
  12.4 0.6 collective-permute-done.rest_2_
  13.0 1.8 %collective-permute-start.17 = (bf16[64,1536]{1,0:T(8,128)(2,1)S(1)}, bf16[64,1536]{1,0:T(8,128)(2,1)S(1)}, u32[]{:S(2)}, u32[]{:S(2)}) collective-permute-start(bf16[64,1536]{1,0:T(8,128)(2,1)S(1)} %shard_map.73.a), channel_id=1, source_target_pairs={{0,4},{2,6},{4,0},{6,2},{8,12},{10,14},{12,8},{14,10},{16,20},{18,... | collective-permute-start | bytes 589832 | tf_op jit(solution)/shard_map/ppermute | solution.py:276
  14.8 3.0 %collective-permute-done.5.rest_3_ = bf16[256,768]{1,0:T(8,128)(2,1)} collective-permute-done((bf16[256,768]{1,0:T(8,128)(2,1)}, bf16[256,768]{1,0:T(8,128)(2,1)}, u32[]{:S(2)}, u32[]{:S(2)}) %collective-permute-start.5) | collective-permute-done | bytes 393248 | tf_op jit(solution)/shard_map/ppermute | solution.py:276
  17.8 0.0 collective-permute-start.6
  17.8 0.0 collective-permute-done.1.rest_3_
  17.8 0.0 collective-permute-start.15
  17.8 6.6 %collective-permute-done.17.b = bf16[64,1536]{1,0:T(8,128)(2,1)S(1)} collective-permute-done((bf16[64,1536]{1,0:T(8,128)(2,1)S(1)}, bf16[64,1536]{1,0:T(8,128)(2,1)S(1)}, u32[]{:S(2)}, u32[]{:S(2)}) %collective-permute-start.17) | collective-permute-done | bytes 196640 | tf_op jit(solution)/shard_map/ppermute | solution.py:276
  24.3 1.3 %collective-permute-start.10 = (bf16[256,768]{1,0:T(8,128)(2,1)}, bf16[256,768]{1,0:T(8,128)(2,1)}, u32[]{:S(2)}, u32[]{:S(2)}) collective-permute-start(bf16[256,768]{1,0:T(8,128)(2,1)} %collective-permute-done.5.rest_3_), channel_id=1, source_target_pairs={{0,4},{2,6},{4,0},{6,2},{8,12},{10,14},{12,8},{14,10},{16,20},{18,... | collective-permute-start | bytes 1179656 | tf_op jit(solution)/shard_map/ppermute | solution.py:276
  25.7 0.0 collective-permute-done.13.rest_1_
  25.7 0.0 copy-start
  25.7 1.7 %collective-permute-start.18 = (bf16[64,1536]{1,0:T(8,128)(2,1)S(1)}, bf16[64,1536]{1,0:T(8,128)(2,1)S(1)}, u32[]{:S(2)}, u32[]{:S(2)}) collective-permute-start(bf16[64,1536]{1,0:T(8,128)(2,1)S(1)} %shard_map.74.a), channel_id=1, source_target_pairs={{0,8},{2,10},{4,12},{6,14},{8,0},{10,2},{12,4},{14,6},{16,24},{18,... | collective-permute-start | bytes 589832 | tf_op jit(solution)/shard_map/ppermute | solution.py:279
  27.4 0.0 collective-permute-done.2.rest_3_
  27.4 0.0 collective-permute-start.14
  27.4 10.0 %collective-permute-done.18.b = bf16[64,1536]{1,0:T(8,128)(2,1)S(1)} collective-permute-done((bf16[64,1536]{1,0:T(8,128)(2,1)S(1)}, bf16[64,1536]{1,0:T(8,128)(2,1)S(1)}, u32[]{:S(2)}, u32[]{:S(2)}) %collective-permute-start.18) | collective-permute-done | bytes 196640 | tf_op jit(solution)/shard_map/ppermute | solution.py:279
  37.4 1.5 %collective-permute-start.3 = (bf16[256,768]{1,0:T(8,128)(2,1)}, bf16[256,768]{1,0:T(8,128)(2,1)S(1)}, u32[]{:S(2)}, u32[]{:S(2)}) collective-permute-start(bf16[256,768]{1,0:T(8,128)(2,1)} %collective-permute-done.2.rest_3_), channel_id=1, source_target_pairs={{0,4},{2,6},{4,0},{6,2},{8,12},{10,14},{12,8},{14,10},{16,20},{18,... | collective-permute-start | bytes 1179656 | tf_op jit(solution)/shard_map/ppermute | solution.py:276
  38.9 0.0 collective-permute-done.6.rest_3_
  38.9 0.5 collective-permute-start.7
  39.5 0.0 collective-permute-done.15.rest_4_
  39.5 0.0 copy-start.2
  39.5 0.6 collective-permute-start.19
  40.1 0.0 collective-permute-done.10.rest_1_
  40.1 0.0 collective-permute-start.12
  40.1 9.8 %collective-permute-done.19.b = bf16[64,1536]{1,0:T(8,128)(2,1)S(1)} collective-permute-done((bf16[64,1536]{1,0:T(8,128)(2,1)S(1)}, bf16[64,1536]{1,0:T(8,128)(2,1)S(1)}, u32[]{:S(2)}, u32[]{:S(2)}) %collective-permute-start.19) | collective-permute-done | bytes 196640 | tf_op jit(solution)/shard_map/ppermute | solution.py:279
  49.9 0.0 collective-permute-start.11
  50.0 0.0 collective-permute-done.14.rest_2_
  50.0 0.0 copy-start.4
  50.0 0.7 copy-done.4
  50.7 0.5 collective-permute-start.20
  51.2 0.0 collective-permute-done.3.rest_1_
  51.2 0.0 copy-done
  51.2 0.1 collective-permute-start.9
  51.3 0.0 copy-done.2
  51.3 5.9 %collective-permute-done.7.rest_1_ = bf16[256,768]{1,0:T(8,128)(2,1)} collective-permute-done((bf16[256,768]{1,0:T(8,128)(2,1)}, bf16[256,768]{1,0:T(8,128)(2,1)}, u32[]{:S(2)}, u32[]{:S(2)}) %collective-permute-start.7) | collective-permute-done | bytes 393248 | tf_op jit(solution)/shard_map/ppermute | solution.py:276
  57.2 0.0 collective-permute-start.8
  57.2 0.0 collective-permute-done.20.rest_2_
  57.2 0.6 collective-permute-start.4
  57.8 4.7 %shard_map.68 = (f32[768,12288]{1,0:T(8,128)}, bf16[768,256]{1,0:T(8,128)(2,1)S(1)}) custom-call(s32[1]{0:T(128)} %bitcast.me, s32[1]{0:T(128)} %bitcast.1.rest_0_, bf16[256,768]{1,0:T(8,128)(2,1)} %bitcast.11, bf16[256,768]{1,0:T(8,128)(2,1)S(1)} %collective-permute-done.rest_2_, bf16[256,768]{1,0:T(8,128)(2,1)S(1)} %collective-permute-done.1.rest_3_, ...), custom_call_target="tpu_custom_call" | custom-call | flops 603979776 | tf_op jit(solution)/shard_map/pallas_call | solution.py:27
  62.5 0.0 slice-done
  62.5 0.0 slice-done.1
  62.5 2.7 %shard_map.77 = (bf16[1024,128]{1,0:T(8,128)(2,1)S(1)}, bf16[1024,128]{1,0:T(8,128)(2,1)S(1)}) custom-call(s32[1]{0:T(128)} %bitcast.me, s32[1]{0:T(128)} %bitcast.3.mine, bf16[2048,1536]{1,0:T(8,128)(2,1)S(1)} %bitcast.5, bf16[64,1536]{1,0:T(8,128)(2,1)S(1)} %shard_map.76.rest_1_, bf16[64,1536]{1,0:T(8,128)(2,1)} %collective-permute-done.20.rest_2_), custom_call_target="tpu_custom_call" | custom-call | tf_op jit(solution)/shard_map/pallas_call | solution.py:27
  65.2 0.0 collective-permute-done.12.rest_4_
  65.2 0.6 collective-permute-start.21
  65.8 0.0 copy-done.1
  65.8 0.0 copy-done.3
  65.8 0.0 copy-done.5
  65.8 7.5 %shard_map.69.rest_6_ = f32[768,12288]{1,0:T(8,128)} custom-call(s32[1]{0:T(128)} %bitcast.me, bf16[768,256]{1,0:T(8,128)(2,1)S(1)} %get-tuple-element.8.rest_0_, bf16[256,768]{1,0:T(8,128)(2,1)S(1)} %copy-done.1, bf16[256,768]{1,0:T(8,128)(2,1)S(1)} %copy-done.5, bf16[256,768]{1,0:T(8,128)(2,1)} %collective-permute-done.5.rest_3_, ...), custom_call_target="tpu_custom_call", output_to_operand_aliasing={{}: (7, {})} | custom-call | flops 1207959552 | tf_op jit(solution)/shard_map/pallas_call | solution.py:27
  73.4 0.0 collective-permute-done.11.rest_2_
  73.4 7.9 %shard_map.70.rest_6_ = f32[768,12288]{1,0:T(8,128)} custom-call(s32[1]{0:T(128)} %bitcast.me, bf16[768,256]{1,0:T(8,128)(2,1)S(1)} %get-tuple-element.8.rest_0_, bf16[256,768]{1,0:T(8,128)(2,1)} %collective-permute-done.10.rest_1_, bf16[256,768]{1,0:T(8,128)(2,1)} %collective-permute-done.11.rest_2_, ...), custom_call_target="tpu_custom_call", output_to_operand_aliasing={{}: (7, {})} | custom-call | flops 1207959552 | tf_op jit(solution)/shard_map/pallas_call | solution.py:27
  81.3 0.0 collective-permute-done.9.rest_4_
  81.3 0.0 collective-permute-done.8.rest_2_
  81.3 7.9 %shard_map.71.rest_4_ = f32[768,12288]{1,0:T(8,128)} custom-call(s32[1]{0:T(128)} %bitcast.me, bf16[768,256]{1,0:T(8,128)(2,1)S(1)} %get-tuple-element.8.rest_0_, bf16[256,768]{1,0:T(8,128)(2,1)} %collective-permute-done.7.rest_1_, bf16[256,768]{1,0:T(8,128)(2,1)} %collective-permute-done.8.rest_2_, ...), custom_call_target="tpu_custom_call", output_to_operand_aliasing={{}: (7, {})} | custom-call | flops 1207959552 | tf_op jit(solution)/shard_map/pallas_call | solution.py:27
  89.2 0.0 collective-permute-done.4.rest_2_
  89.2 0.0 collective-permute-done.21.rest_7_
  89.2 4.1 %shard_map.78 = (f32[768,12288]{1,0:T(8,128)}, f32[1024,128]{1,0:T(8,128)}) custom-call(s32[1]{0:T(128)} %bitcast.me, bf16[768,256]{1,0:T(8,128)(2,1)S(1)} %get-tuple-element.8.rest_0_, bf16[256,768]{1,0:T(8,128)(2,1)S(1)} %collective-permute-done.3.rest_1_, bf16[256,768]{1,0:T(8,128)(2,1)S(1)} %collective-permute-done.4.rest_2_, ...), custom_call_target="tpu_custom_call", output_to_operand_aliasing={{0}: (5, {})} | custom-call | flops 603979776 | tf_op jit(solution)/shard_map/pallas_call | solution.py:27
  (10 shorter events, 0.1 us)
Async XLA Ops:
  0.6 61.8 %slice-start = ((s8[6291456]{0:T(1024)(128)(4,1)}), s8[2097152]{0:T(1024)(128)(4,1)S(1)}, s32[]{:S(2)}) async-start(s8[6291456]{0:T(1024)(128)(4,1)} %bitcast.4), calls=%async_computation | async-start | bytes 4194304
  0.6 12.4 %collective-permute-start = (bf16[256,768]{1,0:T(8,128)(2,1)}, bf16[256,768]{1,0:T(8,128)(2,1)S(1)}, u32[]{:S(2)}, u32[]{:S(2)}) collective-permute-start(bf16[256,768]{1,0:T(8,128)(2,1)} %bitcast.6), channel_id=1, source_target_pairs={{0,1},{1,0},{2,3},{3,2},{4,5},{5,4},{6,7},{7,6},{8,9},{9,8},{10,11... | collective-permute-start | bytes 1179656 | tf_op jit(solution)/shard_map/ppermute | solution.py:298
  3.7 14.1 %collective-permute-start.5 = (bf16[256,768]{1,0:T(8,128)(2,1)}, bf16[256,768]{1,0:T(8,128)(2,1)}, u32[]{:S(2)}, u32[]{:S(2)}) collective-permute-start(bf16[256,768]{1,0:T(8,128)(2,1)} %bitcast.7), channel_id=1, source_target_pairs={{0,8},{2,10},{4,12},{6,14},{8,16},{10,18},{12,20},{14,22},{16,24},... | collective-permute-start | bytes 1179656 | tf_op jit(solution)/shard_map/ppermute | solution.py:276
  5.3 12.5 %collective-permute-start.1 = (bf16[256,768]{1,0:T(8,128)(2,1)}, bf16[256,768]{1,0:T(8,128)(2,1)S(1)}, u32[]{:S(2)}, u32[]{:S(2)}) collective-permute-start(bf16[256,768]{1,0:T(8,128)(2,1)} %bitcast.8), channel_id=1, source_target_pairs={{0,2},{2,0},{4,6},{6,4},{8,10},{10,8},{12,14},{14,12},{16,18},{18,... | collective-permute-start | bytes 1179656 | tf_op jit(solution)/shard_map/ppermute | solution.py:276
  5.3 0.7 copy-start.6
  8.2 2.0 %collective-permute-start.16 = (bf16[64,1536]{1,0:T(8,128)(2,1)S(1)}, bf16[64,1536]{1,0:T(8,128)(2,1)S(1)}, u32[]{:S(2)}, u32[]{:S(2)}) collective-permute-start(bf16[64,1536]{1,0:T(8,128)(2,1)S(1)} %get-tuple-element.11), channel_id=1, source_target_pairs={{0,2},{2,0},{4,6},{6,4},{8,10},{10,8},{12,14},{14,12},{16,18},{18,... | collective-permute-start | bytes 589832 | tf_op jit(solution)/shard_map/ppermute | solution.py:276
  8.8 16.8 %collective-permute-start.13 = (bf16[256,768]{1,0:T(8,128)(2,1)}, bf16[256,768]{1,0:T(8,128)(2,1)S(1)}, u32[]{:S(2)}, u32[]{:S(2)}) collective-permute-start(bf16[256,768]{1,0:T(8,128)(2,1)} %bitcast.9), channel_id=1, source_target_pairs={{0,4},{2,6},{4,0},{6,2},{8,12},{10,14},{12,8},{14,10},{16,20},{18,... | collective-permute-start | bytes 1179656 | tf_op jit(solution)/shard_map/ppermute | solution.py:276
  10.1 17.3 %collective-permute-start.2 = (bf16[256,768]{1,0:T(8,128)(2,1)}, bf16[256,768]{1,0:T(8,128)(2,1)}, u32[]{:S(2)}, u32[]{:S(2)}) collective-permute-start(bf16[256,768]{1,0:T(8,128)(2,1)} %bitcast.10), channel_id=1, source_target_pairs={{0,24},{2,26},{4,28},{6,30},{8,0},{10,2},{12,4},{14,6},{16,8},{18,... | collective-permute-start | bytes 1179656 | tf_op jit(solution)/shard_map/ppermute | solution.py:276
  13.0 11.3 %collective-permute-start.17 = (bf16[64,1536]{1,0:T(8,128)(2,1)S(1)}, bf16[64,1536]{1,0:T(8,128)(2,1)S(1)}, u32[]{:S(2)}, u32[]{:S(2)}) collective-permute-start(bf16[64,1536]{1,0:T(8,128)(2,1)S(1)} %shard_map.73.a), channel_id=1, source_target_pairs={{0,4},{2,6},{4,0},{6,2},{8,12},{10,14},{12,8},{14,10},{16,20},{18,... | collective-permute-start | bytes 589832 | tf_op jit(solution)/shard_map/ppermute | solution.py:276
  17.8 21.2 %collective-permute-start.6 = (bf16[256,768]{1,0:T(8,128)(2,1)}, bf16[256,768]{1,0:T(8,128)(2,1)}, u32[]{:S(2)}, u32[]{:S(2)}) collective-permute-start(bf16[256,768]{1,0:T(8,128)(2,1)} %collective-permute-done.5.rest_3_), channel_id=1, source_target_pairs={{0,8},{2,10},{4,12},{6,14},{8,16},{10,18},{12,20},{14,22},{16,24},... | collective-permute-start | bytes 1179656 | tf_op jit(solution)/shard_map/ppermute | solution.py:276
  17.8 21.7 %collective-permute-start.15 = (bf16[256,768]{1,0:T(8,128)(2,1)}, bf16[256,768]{1,0:T(8,128)(2,1)S(1)}, u32[]{:S(2)}, u32[]{:S(2)}) collective-permute-start(bf16[256,768]{1,0:T(8,128)(2,1)} %collective-permute-done.5.rest_3_), channel_id=1, source_target_pairs={{0,2},{2,0},{4,6},{6,4},{8,10},{10,8},{12,14},{14,12},{16,18},{18,... | collective-permute-start | bytes 1179656 | tf_op jit(solution)/shard_map/ppermute | solution.py:276
  24.3 15.8 %collective-permute-start.10 = (bf16[256,768]{1,0:T(8,128)(2,1)}, bf16[256,768]{1,0:T(8,128)(2,1)}, u32[]{:S(2)}, u32[]{:S(2)}) collective-permute-start(bf16[256,768]{1,0:T(8,128)(2,1)} %collective-permute-done.5.rest_3_), channel_id=1, source_target_pairs={{0,4},{2,6},{4,0},{6,2},{8,12},{10,14},{12,8},{14,10},{16,20},{18,... | collective-permute-start | bytes 1179656 | tf_op jit(solution)/shard_map/ppermute | solution.py:276
  25.7 25.6 %copy-start = (bf16[256,768]{1,0:T(8,128)(2,1)}, bf16[256,768]{1,0:T(8,128)(2,1)S(1)}, u32[]{:S(2)}) copy-start(bf16[256,768]{1,0:T(8,128)(2,1)S(1)} %collective-permute-done.13.rest_1_) | copy-start | bytes 1179652
  25.7 11.7 %collective-permute-start.18 = (bf16[64,1536]{1,0:T(8,128)(2,1)S(1)}, bf16[64,1536]{1,0:T(8,128)(2,1)S(1)}, u32[]{:S(2)}, u32[]{:S(2)}) collective-permute-start(bf16[64,1536]{1,0:T(8,128)(2,1)S(1)} %shard_map.74.a), channel_id=1, source_target_pairs={{0,8},{2,10},{4,12},{6,14},{8,0},{10,2},{12,4},{14,6},{16,24},{18,... | collective-permute-start | bytes 589832 | tf_op jit(solution)/shard_map/ppermute | solution.py:279
  27.4 22.6 %collective-permute-start.14 = (bf16[256,768]{1,0:T(8,128)(2,1)S(1)}, bf16[256,768]{1,0:T(8,128)(2,1)S(1)}, u32[]{:S(2)}, u32[]{:S(2)}) collective-permute-start(bf16[256,768]{1,0:T(8,128)(2,1)S(1)} %collective-permute-done.13.rest_1_), channel_id=1, source_target_pairs={{0,2},{2,0},{4,6},{6,4},{8,10},{10,8},{12,14},{14,12},{16,18},{18,... | collective-permute-start | bytes 1179656 | tf_op jit(solution)/shard_map/ppermute | solution.py:276
  37.4 13.8 %collective-permute-start.3 = (bf16[256,768]{1,0:T(8,128)(2,1)}, bf16[256,768]{1,0:T(8,128)(2,1)S(1)}, u32[]{:S(2)}, u32[]{:S(2)}) collective-permute-start(bf16[256,768]{1,0:T(8,128)(2,1)} %collective-permute-done.2.rest_3_), channel_id=1, source_target_pairs={{0,4},{2,6},{4,0},{6,2},{8,12},{10,14},{12,8},{14,10},{16,20},{18,... | collective-permute-start | bytes 1179656 | tf_op jit(solution)/shard_map/ppermute | solution.py:276
  38.9 18.3 %collective-permute-start.7 = (bf16[256,768]{1,0:T(8,128)(2,1)}, bf16[256,768]{1,0:T(8,128)(2,1)}, u32[]{:S(2)}, u32[]{:S(2)}) collective-permute-start(bf16[256,768]{1,0:T(8,128)(2,1)} %collective-permute-done.6.rest_3_), channel_id=1, source_target_pairs={{0,4},{2,6},{4,0},{6,2},{8,12},{10,14},{12,8},{14,10},{16,20},{18,... | collective-permute-start | bytes 1179656 | tf_op jit(solution)/shard_map/ppermute | solution.py:276
  39.5 11.8 %copy-start.2 = (bf16[256,768]{1,0:T(8,128)(2,1)}, bf16[256,768]{1,0:T(8,128)(2,1)S(1)}, u32[]{:S(2)}) copy-start(bf16[256,768]{1,0:T(8,128)(2,1)S(1)} %collective-permute-done.15.rest_4_) | copy-start | bytes 1179652
  39.5 10.4 %collective-permute-start.19 = (bf16[64,1536]{1,0:T(8,128)(2,1)S(1)}, bf16[64,1536]{1,0:T(8,128)(2,1)S(1)}, u32[]{:S(2)}, u32[]{:S(2)}) collective-permute-start(bf16[64,1536]{1,0:T(8,128)(2,1)S(1)} %shard_map.75.a), channel_id=1, source_target_pairs={{0,16},{2,18},{4,20},{6,22},{8,24},{10,26},{12,28},{14,30},{16,0},... | collective-permute-start | bytes 589832 | tf_op jit(solution)/shard_map/ppermute | solution.py:279
  40.1 25.1 %collective-permute-start.12 = (bf16[256,768]{1,0:T(8,128)(2,1)}, bf16[256,768]{1,0:T(8,128)(2,1)}, u32[]{:S(2)}, u32[]{:S(2)}) collective-permute-start(bf16[256,768]{1,0:T(8,128)(2,1)} %collective-permute-done.6.rest_3_), channel_id=1, source_target_pairs={{0,2},{2,0},{4,6},{6,4},{8,10},{10,8},{12,14},{14,12},{16,18},{18,... | collective-permute-start | bytes 1179656 | tf_op jit(solution)/shard_map/ppermute | solution.py:276
  49.9 23.5 %collective-permute-start.11 = (bf16[256,768]{1,0:T(8,128)(2,1)}, bf16[256,768]{1,0:T(8,128)(2,1)}, u32[]{:S(2)}, u32[]{:S(2)}) collective-permute-start(bf16[256,768]{1,0:T(8,128)(2,1)} %collective-permute-done.10.rest_1_), channel_id=1, source_target_pairs={{0,2},{2,0},{4,6},{6,4},{8,10},{10,8},{12,14},{14,12},{16,18},{18,... | collective-permute-start | bytes 1179656 | tf_op jit(solution)/shard_map/ppermute | solution.py:276
  50.0 0.8 copy-start.4
  50.7 6.5 %collective-permute-start.20 = (bf16[64,1536]{1,0:T(8,128)(2,1)S(1)}, bf16[64,1536]{1,0:T(8,128)(2,1)}, u32[]{:S(2)}, u32[]{:S(2)}) collective-permute-start(bf16[64,1536]{1,0:T(8,128)(2,1)S(1)} %shard_map.76.rest_1_), channel_id=1, source_target_pairs={{0,2},{2,0},{4,6},{6,4},{8,10},{10,8},{12,14},{14,12},{16,18},{18,... | collective-permute-start | bytes 589832 | tf_op jit(solution)/shard_map/ppermute | solution.py:276
  51.2 30.1 %collective-permute-start.9 = (bf16[256,768]{1,0:T(8,128)(2,1)}, bf16[256,768]{1,0:T(8,128)(2,1)}, u32[]{:S(2)}, u32[]{:S(2)}) collective-permute-start(bf16[256,768]{1,0:T(8,128)(2,1)} %collective-permute-done.2.rest_3_), channel_id=1, source_target_pairs={{0,2},{2,0},{4,6},{6,4},{8,10},{10,8},{12,14},{14,12},{16,18},{18,... | collective-permute-start | bytes 1179656 | tf_op jit(solution)/shard_map/ppermute | solution.py:276
  57.2 24.1 %collective-permute-start.8 = (bf16[256,768]{1,0:T(8,128)(2,1)}, bf16[256,768]{1,0:T(8,128)(2,1)}, u32[]{:S(2)}, u32[]{:S(2)}) collective-permute-start(bf16[256,768]{1,0:T(8,128)(2,1)} %collective-permute-done.7.rest_1_), channel_id=1, source_target_pairs={{0,2},{2,0},{4,6},{6,4},{8,10},{10,8},{12,14},{14,12},{16,18},{18,... | collective-permute-start | bytes 1179656 | tf_op jit(solution)/shard_map/ppermute | solution.py:276
  57.2 8.6 %copy-start.1 = (bf16[256,768]{1,0:T(8,128)(2,1)S(1)}, bf16[256,768]{1,0:T(8,128)(2,1)}, u32[]{:S(2)}) copy-start(bf16[256,768]{1,0:T(8,128)(2,1)} %copy-done) | copy-start | bytes 1179652
  57.2 8.6 %copy-start.3 = (bf16[256,768]{1,0:T(8,128)(2,1)S(1)}, bf16[256,768]{1,0:T(8,128)(2,1)}, u32[]{:S(2)}) copy-start(bf16[256,768]{1,0:T(8,128)(2,1)} %copy-done.2) | copy-start | bytes 1179652
  57.2 8.6 %copy-start.5 = (bf16[256,768]{1,0:T(8,128)(2,1)S(1)}, bf16[256,768]{1,0:T(8,128)(2,1)}, u32[]{:S(2)}) copy-start(bf16[256,768]{1,0:T(8,128)(2,1)} %copy-done.4) | copy-start | bytes 1179652
  57.2 32.0 %collective-permute-start.4 = (bf16[256,768]{1,0:T(8,128)(2,1)S(1)}, bf16[256,768]{1,0:T(8,128)(2,1)S(1)}, u32[]{:S(2)}, u32[]{:S(2)}) collective-permute-start(bf16[256,768]{1,0:T(8,128)(2,1)S(1)} %collective-permute-done.3.rest_1_), channel_id=1, source_target_pairs={{0,2},{2,0},{4,6},{6,4},{8,10},{10,8},{12,14},{14,12},{16,18},{18,... | collective-permute-start | bytes 1179656 | tf_op jit(solution)/shard_map/ppermute | solution.py:276
  57.8 4.7 %slice-start.1 = ((s8[6291456]{0:T(1024)(128)(4,1)}), s8[4194304]{0:T(1024)(128)(4,1)S(1)}, s32[]{:S(2)}) async-start(s8[6291456]{0:T(1024)(128)(4,1)} %bitcast.4), calls=%async_computation.1 | async-start | bytes 8388608
  65.2 24.0 %collective-permute-start.21 = (bf16[1024,128]{1,0:T(8,128)(2,1)S(1)}, bf16[1024,128]{1,0:T(8,128)(2,1)S(1)}, u32[]{:S(2)}, u32[]{:S(2)}) collective-permute-start(bf16[1024,128]{1,0:T(8,128)(2,1)S(1)} %get-tuple-element.13), channel_id=1, source_target_pairs={{0,1},{1,0},{2,3},{3,2},{4,5},{5,4},{6,7},{7,6},{8,9},{9,8},{10,11... | collective-permute-start | bytes 786440 | tf_op jit(solution)/shard_map/ppermute | solution.py:340

commit v3 on v2

--- a/solution.py
+++ b/solution.py
@@ -14,6 +14,7 @@
     return n // (core * near), near, core
 
 
+HELD = 0
 HBM = pl.BlockSpec(memory_space=pltpu.HBM)
 VMEM = pl.BlockSpec(memory_space=pltpu.VMEM)
 SMEM = pl.BlockSpec(memory_space=pltpu.SMEM)
@@ -36,41 +37,77 @@
     )(*operands)
 
 
-def update_kernel(me, *rest, spots, extent, tiles, first, tail):
+def window(me, spots, extent, high, width):
     far, near, cores = extent
+    z, y, c = me[0] // (near * cores), me[0] // cores % near, me[0] % cores
+
+    def spot(at, tile):
+        a, b, d = spots[at]
+        column = (((z + a + far) % far * near) + (y + b) % near) * cores + (c + d) % cores
+        return pl.ds(tile * high, high), pl.ds(pl.multiple_of(column * width, 128), width)
+
+    return spot
+
+
+def hold_kernel(me, own, old, before, mine, arrive, here, *, spots, extent, tiles):
+    high, width = before.shape[1:]
+    spot = window(me, spots, extent, high, width)
+    copies = [pltpu.make_async_copy(own, mine, here)]
+    for n in range(len(spots) * tiles):
+        copies.append(pltpu.make_async_copy(old.at[spot(n // tiles, n % tiles)], before.at[n], arrive.at[n]))
+    for copy in copies:
+        copy.start()
+    for copy in copies:
+        copy.wait()
+
+
+def row_tiles(rows):
+    return next(t for t in (2, 1) if rows % (8 * t) == 0)
+
+
+def hold(me, own, old, spots, extent):
+    tiles = row_tiles(old.shape[0])
+    count = len(spots) * tiles
+    return call(
+        functools.partial(hold_kernel, spots=spots, extent=extent, tiles=tiles),
+        [
+            jax.ShapeDtypeStruct((count, old.shape[0] // tiles, own.shape[1]), old.dtype),
+            jax.ShapeDtypeStruct(own.shape, own.dtype),
+        ],
+        [me, keep(own), keep(old)],
+        [SMEM, HBM, HBM],
+        [VMEM, VMEM],
+        scratch=[pltpu.SemaphoreType.DMA((count,)), pltpu.SemaphoreType.DMA],
+    )
+
+
+def update_kernel(me, *rest, spots, extent, tiles, first, tail, ready, skip):
     count = len(spots)
     if tail:
         rest, (total, pair_in, pair_out) = rest[:-3], rest[-3:]
     held, arrive, leave = rest[-3:]
     high, width = held.shape[1:]
-    z, y, c = me[0] // (near * cores), me[0] // cores % near, me[0] % cores
     pieces = [(at, tile) for at in range(count) for tile in range(tiles)]
     lag = 3 if len(pieces) >= 8 else 0
+    spot = window(me, spots, extent, high, width)
+    if ready:
+        before, rest = rest[0], rest[1:]
     if first:
-        mask, own, got, *blocks = rest[: count + 2]
-        old, out, slab, mine, here = rest[count + 2 : count + 7]
-        blocks = [mine, *blocks]
+        mask, got, *blocks = rest[: count + 2]
+        old, out, slab = rest[count + 2 : count + 5]
     else:
         slab, *blocks = rest[: count + 1]
         old = rest[count + 1]
         pair, *parts = rest[count + 3 : count + 3 + tail] if tail else [None]
         out = rest[count + 3 + tail]
 
-    def spot(at, tile):
-        a, b, d = spots[at]
-        column = (((z + a + far) % far * near) + (y + b) % near) * cores + (c + d) % cores
-        return pl.ds(tile * high, high), pl.ds(pl.multiple_of(column * width, 128), width)
-
     def load(n):
         return pltpu.make_async_copy(old.at[spot(*pieces[n])], held.at[n], arrive.at[n])
 
     def save(n):
         return pltpu.make_async_copy(held.at[n], out.at[spot(*pieces[n])], leave.at[n])
 
-    if first:
-        bring = pltpu.make_async_copy(own, mine, here)
-        bring.start()
-    for n in range(len(pieces)):
+    for n in range(ready, len(pieces)):
         load(n).start()
     if tail:
         residual = rest[count + 4 + tail]
@@ -78,12 +115,13 @@
         pair_save = pltpu.make_async_copy(total, residual, pair_out)
         pair_load.start()
     if first:
-        bring.wait()
-        chosen = jnp.where(mask[0] != 0, got[...].astype(jnp.float32), mine[...].astype(jnp.float32))
+        chosen = jnp.where(mask[0] != 0, got[...].astype(jnp.float32), blocks[0][...].astype(jnp.float32))
         slab[...] = chosen.T.astype(slab.dtype)
     for n, (at, tile) in enumerate(pieces):
-        load(n).wait()
-        held[n] += jnp.dot(
+        if n >= ready:
+            load(n).wait()
+        start = before[skip + n] if n < ready else held[n]
+        held[n] = start + jnp.dot(
             slab[tile * high : (tile + 1) * high, :], blocks[at][...], preferred_element_type=jnp.float32
         )
         if n >= lag:
@@ -103,13 +141,14 @@
         save(n).wait()
 
 
-def update(me, rows_of, old, blocks, spots, extent, target, tail=()):
+def update(me, rows_of, old, blocks, spots, extent, target, tail=(), before=None, ready=0, skip=0):
     first = target is None
     inner, width = blocks[-1].shape
     rows = old.shape[0]
     count = len(blocks)
-    tiles = next(t for t in (2, 1) if rows % (8 * t) == 0)
+    tiles = row_tiles(rows)
     high = rows // tiles
+    early = [before] if ready else []
     shape = jax.ShapeDtypeStruct(old.shape, old.dtype)
     scratch = [
         pltpu.VMEM((count * tiles, high, width), old.dtype),
@@ -118,15 +157,14 @@
     ]
     if first:
         mask, got = rows_of
-        operands = [me, mask, keep(blocks[0]), got, *blocks[1:], keep(old)]
-        specs = [SMEM, SMEM, HBM, VMEM] + [VMEM] * (count - 1) + [HBM]
+        operands = [me, *early, mask, got, *blocks, keep(old)]
+        specs = [SMEM] + [VMEM] * len(early) + [SMEM, VMEM] + [VMEM] * count + [HBM]
         aliases = {}
         outs = [shape, jax.ShapeDtypeStruct((rows, inner), got.dtype)]
         out_specs = [HBM, VMEM]
-        scratch = [pltpu.VMEM((inner, width), got.dtype), pltpu.SemaphoreType.DMA] + scratch
     else:
-        operands = [me, rows_of, *blocks, keep(old), target]
-        specs = [SMEM, VMEM] + [VMEM] * count + [HBM, HBM]
+        operands = [me, *early, rows_of, *blocks, keep(old), target]
+        specs = [SMEM] + [VMEM] * len(early) + [VMEM] + [VMEM] * count + [HBM, HBM]
         aliases = {len(operands) - 1: 0}
         outs, out_specs = [shape], [HBM]
         if tail:
@@ -140,7 +178,7 @@
                 pltpu.SemaphoreType.DMA,
             ]
     return call(
-        functools.partial(update_kernel, spots=spots, extent=extent, tiles=tiles, first=first, tail=len(tail)),
+        functools.partial(update_kernel, spots=spots, extent=extent, tiles=tiles, first=first, tail=len(tail), ready=ready * tiles, skip=skip * tiles),
         outs,
         operands,
         specs,
@@ -343,6 +381,8 @@
         new_block = None
         order = batches(far, near, cores)
         rows_of = (takes.astype(jnp.int32)[None], got)
+        early = order[0] + order[1][:HELD]
+        before, blocks[0] = hold(me[None], own, old_block, [spots[at] for at in early], (far, near, cores))
         for number, batch in enumerate(order):
             done = update(
                 me[None],
@@ -353,6 +393,9 @@
                 (far, near, cores),
                 new_block,
                 (pair_columns, parts[-1], *arrived) if batch == order[-1] else (),
+                before,
+                (len(order[0]), min(HELD, len(order[1])))[number] if number < 2 else 0,
+                len(order[0]) * number,
             )
             new_block = done[0]
             if number == 0:

time: 93.7 us -> 101 us (1.078)
  local copies, waits for them, and re-layouts: 1.47 us -> 8.6 us
    unnamed x18 -> x30, local copies, waits for them, and re-layouts: 1.47 us -> 8.6 us
    pallas_call x11 -> x12, Pallas kernels: 37.1 us -> 37.1 us  [call(): pl.pallas_call(kernel, out_shape=out_shape, in_specs=specs, out_specs=out...]
  transfers between devices with their start and end apart: 22 -> 22, of which waited for: 6 -> 6; matrix products, arithmetic and copies ran while one was open for 0% -> 0% of each run, Pallas kernels for 35% -> 33%
where the time goes in v3:
time: 101 us; the launch traced here: 100 us
  Pallas kernels  37.1 us (37%)
  waiting for transfers between devices  35.9 us (36%)
  starting transfers between devices  17.9 us (18%)
  local copies, waits for them, and re-layouts  8.6 us (9%)
    pallas_call x12, Pallas kernels, call(): pl.pallas_call(kernel, out_shape=out_shape, in_specs=specs, out_specs=out...  37.1 us
    ppermute x2, waiting for transfers between devices, swap_far(): lax.ppermute(x, 'gx', [(place(i, j, k), place(i ^ bit, j, k)) for i, j, k...  19.8 us
    ppermute x18, waiting for transfers between devices, shift(): lax.ppermute(x, 'gx', [(place(i, j, k), place(i + a, j + b, k + d)) for i...  15.5 us
    ppermute x18, starting transfers between devices, shift(): lax.ppermute(x, 'gx', [(place(i, j, k), place(i + a, j + b, k + d)) for i...  12 us
    unnamed x30, local copies, waits for them, and re-layouts  8.6 us
    ppermute x1, starting transfers between devices, local(): lax.ppermute(slab, 'gy', [(g, (g + reach) % groups) for g in range(groups)])  3.03 us
    ppermute x2, starting transfers between devices, swap_far(): lax.ppermute(x, 'gx', [(place(i, j, k), place(i ^ bit, j, k)) for i, j, k...  2.32 us
  transfers between devices with their start and end apart: 22, of which 6 were waited for; matrix products, arithmetic and copies ran while one was open for 0% of the time, Pallas kernels for 33%

profile of v3, /device:TPU:0, one launch (start us, length us, event | category | flops | bytes accessed | tf_op | source)
XLA Modules:
  0.0 100.4 jit_solution(945336488826724864)
XLA Ops:
  0.6 3.0 %collective-permute-start = (bf16[256,768]{1,0:T(8,128)(2,1)}, bf16[256,768]{1,0:T(8,128)(2,1)S(1)}, u32[]{:S(2)}, u32[]{:S(2)}) collective-permute-start(bf16[256,768]{1,0:T(8,128)(2,1)} %bitcast.6), channel_id=1, source_target_pairs={{0,1},{1,0},{2,3},{3,2},{4,5},{5,4},{6,7},{7,6},{8,9},{9,8},{10,11... | collective-permute-start | bytes 1179656 | tf_op jit(solution)/shard_map/ppermute | solution.py:336
  3.7 1.6 %collective-permute-start.5 = (bf16[256,768]{1,0:T(8,128)(2,1)}, bf16[256,768]{1,0:T(8,128)(2,1)S(1)}, u32[]{:S(2)}, u32[]{:S(2)}) collective-permute-start(bf16[256,768]{1,0:T(8,128)(2,1)} %bitcast.7), channel_id=1, source_target_pairs={{0,8},{2,10},{4,12},{6,14},{8,16},{10,18},{12,20},{14,22},{16,24},... | collective-permute-start | bytes 1179656 | tf_op jit(solution)/shard_map/ppermute | solution.py:314
  5.2 0.0 collective-permute-start.1
  5.2 0.7 copy-done.12
  5.9 2.2 %shard_map.73 = (bf16[64,1536]{1,0:T(8,128)(2,1)S(1)}, bf16[64,1536]{1,0:T(8,128)(2,1)S(1)}) custom-call(s32[128]{0:T(128)S(1)} %copy-done.12, s32[1]{0:T(128)} %bitcast.me, bf16[2048,1536]{1,0:T(8,128)(2,1)} %rest_0_.1), custom_call_target="tpu_custom_call" | custom-call | tf_op jit(solution)/shard_map/pallas_call | solution.py:28
  8.1 0.7 collective-permute-start.16
  8.8 1.3 %collective-permute-start.13 = (bf16[256,768]{1,0:T(8,128)(2,1)}, bf16[256,768]{1,0:T(8,128)(2,1)S(1)}, u32[]{:S(2)}, u32[]{:S(2)}) collective-permute-start(bf16[256,768]{1,0:T(8,128)(2,1)} %bitcast.9), channel_id=1, source_target_pairs={{0,4},{2,6},{4,0},{6,2},{8,12},{10,14},{12,8},{14,10},{16,20},{18,... | collective-permute-start | bytes 1179656 | tf_op jit(solution)/shard_map/ppermute | solution.py:314
  10.1 0.0 collective-permute-done.16.b
  10.1 2.2 %collective-permute-start.2 = (bf16[256,768]{1,0:T(8,128)(2,1)}, bf16[256,768]{1,0:T(8,128)(2,1)}, u32[]{:S(2)}, u32[]{:S(2)}) collective-permute-start(bf16[256,768]{1,0:T(8,128)(2,1)} %bitcast.10), channel_id=1, source_target_pairs={{0,24},{2,26},{4,28},{6,30},{8,0},{10,2},{12,4},{14,6},{16,8},{18,... | collective-permute-start | bytes 1179656 | tf_op jit(solution)/shard_map/ppermute | solution.py:314
  12.4 0.6 collective-permute-done.rest_2_
  13.0 1.8 %collective-permute-start.17 = (bf16[64,1536]{1,0:T(8,128)(2,1)S(1)}, bf16[64,1536]{1,0:T(8,128)(2,1)S(1)}, u32[]{:S(2)}, u32[]{:S(2)}) collective-permute-start(bf16[64,1536]{1,0:T(8,128)(2,1)S(1)} %shard_map.74.a), channel_id=1, source_target_pairs={{0,4},{2,6},{4,0},{6,2},{8,12},{10,14},{12,8},{14,10},{16,20},{18,... | collective-permute-start | bytes 589832 | tf_op jit(solution)/shard_map/ppermute | solution.py:314
  14.8 2.9 %collective-permute-done.5.rest_3_ = bf16[256,768]{1,0:T(8,128)(2,1)S(1)} collective-permute-done((bf16[256,768]{1,0:T(8,128)(2,1)}, bf16[256,768]{1,0:T(8,128)(2,1)S(1)}, u32[]{:S(2)}, u32[]{:S(2)}) %collective-permute-start.5) | collective-permute-done | bytes 393248 | tf_op jit(solution)/shard_map/ppermute | solution.py:314
  17.6 0.0 collective-permute-start.6
  17.6 0.0 collective-permute-done.1.rest_4_
  17.7 0.1 collective-permute-start.15
  17.7 6.6 %collective-permute-done.17.b = bf16[64,1536]{1,0:T(8,128)(2,1)S(1)} collective-permute-done((bf16[64,1536]{1,0:T(8,128)(2,1)S(1)}, bf16[64,1536]{1,0:T(8,128)(2,1)S(1)}, u32[]{:S(2)}, u32[]{:S(2)}) %collective-permute-start.17) | collective-permute-done | bytes 196640 | tf_op jit(solution)/shard_map/ppermute | solution.py:314
  24.3 1.3 %collective-permute-start.10 = (bf16[256,768]{1,0:T(8,128)(2,1)S(1)}, bf16[256,768]{1,0:T(8,128)(2,1)}, u32[]{:S(2)}, u32[]{:S(2)}) collective-permute-start(bf16[256,768]{1,0:T(8,128)(2,1)S(1)} %collective-permute-done.5.rest_3_), channel_id=1, source_target_pairs={{0,4},{2,6},{4,0},{6,2},{8,12},{10,14},{12,8},{14,10},{16,20},{18,... | collective-permute-start | bytes 1179656 | tf_op jit(solution)/shard_map/ppermute | solution.py:314
  25.6 0.0 collective-permute-done.13.rest_1_
  25.7 0.0 copy-start.6
  25.7 1.7 %collective-permute-start.18 = (bf16[64,1536]{1,0:T(8,128)(2,1)S(1)}, bf16[64,1536]{1,0:T(8,128)(2,1)S(1)}, u32[]{:S(2)}, u32[]{:S(2)}) collective-permute-start(bf16[64,1536]{1,0:T(8,128)(2,1)S(1)} %shard_map.75.a), channel_id=1, source_target_pairs={{0,8},{2,10},{4,12},{6,14},{8,0},{10,2},{12,4},{14,6},{16,24},{18,... | collective-permute-start | bytes 589832 | tf_op jit(solution)/shard_map/ppermute | solution.py:317
  27.4 0.0 collective-permute-done.2.rest_3_
  27.4 0.0 collective-permute-start.14
  27.4 10.0 %collective-permute-done.18.b = bf16[64,1536]{1,0:T(8,128)(2,1)S(1)} collective-permute-done((bf16[64,1536]{1,0:T(8,128)(2,1)S(1)}, bf16[64,1536]{1,0:T(8,128)(2,1)S(1)}, u32[]{:S(2)}, u32[]{:S(2)}) %collective-permute-start.18) | collective-permute-done | bytes 196640 | tf_op jit(solution)/shard_map/ppermute | solution.py:317
  37.4 1.5 %collective-permute-start.3 = (bf16[256,768]{1,0:T(8,128)(2,1)}, bf16[256,768]{1,0:T(8,128)(2,1)S(1)}, u32[]{:S(2)}, u32[]{:S(2)}) collective-permute-start(bf16[256,768]{1,0:T(8,128)(2,1)} %collective-permute-done.2.rest_3_), channel_id=1, source_target_pairs={{0,4},{2,6},{4,0},{6,2},{8,12},{10,14},{12,8},{14,10},{16,20},{18,... | collective-permute-start | bytes 1179656 | tf_op jit(solution)/shard_map/ppermute | solution.py:314
  38.9 0.0 collective-permute-done.6.rest_3_
  38.9 0.5 collective-permute-start.7
  39.5 0.0 collective-permute-done.15.rest_4_
  39.5 0.0 copy-start.8
  39.5 0.6 collective-permute-start.19
  40.1 0.0 collective-permute-done.10.rest_1_
  40.1 0.0 collective-permute-start.12
  40.1 9.8 %collective-permute-done.19.b = bf16[64,1536]{1,0:T(8,128)(2,1)S(1)} collective-permute-done((bf16[64,1536]{1,0:T(8,128)(2,1)S(1)}, bf16[64,1536]{1,0:T(8,128)(2,1)S(1)}, u32[]{:S(2)}, u32[]{:S(2)}) %collective-permute-start.19) | collective-permute-done | bytes 196640 | tf_op jit(solution)/shard_map/ppermute | solution.py:317
  49.9 0.0 collective-permute-start.11
  49.9 0.0 collective-permute-done.14.rest_2_
  50.0 0.7 copy-done.10
  50.7 0.5 collective-permute-start.20
  51.2 0.0 collective-permute-done.3.rest_1_
  51.2 0.0 collective-permute-start.9
  51.2 6.0 %collective-permute-done.7.rest_1_ = bf16[256,768]{1,0:T(8,128)(2,1)} collective-permute-done((bf16[256,768]{1,0:T(8,128)(2,1)}, bf16[256,768]{1,0:T(8,128)(2,1)}, u32[]{:S(2)}, u32[]{:S(2)}) %collective-permute-start.7) | collective-permute-done | bytes 393248 | tf_op jit(solution)/shard_map/ppermute | solution.py:314
  57.2 0.0 collective-permute-start.8
  57.2 0.0 copy-done.4
  57.2 0.0 slice-start
  57.2 2.7 %shard_map.68 = (f32[4,384,768]{2,1,0:T(8,128)S(1)}, bf16[256,768]{1,0:T(8,128)(2,1)S(1)}) custom-call(s32[1]{0:T(128)} %bitcast.me, bf16[256,768]{1,0:T(8,128)(2,1)} %bitcast.11, f32[768,12288]{1,0:T(8,128)} %rest_3_.1), custom_call_target="tpu_custom_call" | custom-call | tf_op jit(solution)/shard_map/pallas_call | solution.py:28
  59.9 0.0 copy-start
  59.9 2.2 %copy-done = f32[4,384,768]{2,1,0:T(8,128)} copy-done((f32[4,384,768]{2,1,0:T(8,128)}, f32[4,384,768]{2,1,0:T(8,128)S(1)}, u32[]{:S(2)}) %copy-start) | copy-done | bytes 4718616
  62.1 0.7 copy-done.2
  62.8 0.0 collective-permute-done.20.rest_2_
  62.8 0.5 collective-permute-start.4
  63.3 2.3 %copy-done.1 = f32[4,384,768]{2,1,0:T(8,128)S(1)} copy-done((f32[4,384,768]{2,1,0:T(8,128)S(1)}, f32[4,384,768]{2,1,0:T(8,128)}, u32[]{:S(2)}) %copy-start.1) | copy-done | bytes 4718616
  65.7 1.0 copy-done.3
  66.7 2.9 %shard_map.69 = (f32[768,12288]{1,0:T(8,128)}, bf16[768,256]{1,0:T(8,128)(2,1)S(1)}) custom-call(s32[1]{0:T(128)} %bitcast.me, f32[4,384,768]{2,1,0:T(8,128)S(1)} %copy-done.1, s32[1]{0:T(128)} %bitcast.2.rest_1_, bf16[256,768]{1,0:T(8,128)(2,1)S(1)} %collective-permute-done.rest_2_, bf16[256,768]{1,0:T(8,128)(2,1)S(1)} %copy-done.3, ...), custom_call_target="tpu_custom_call" | custom-call | flops 603979776 | tf_op jit(solution)/shard_map/pallas_call | solution.py:28
  69.7 0.9 slice-done.1
  70.6 2.7 %shard_map.78 = (bf16[1024,128]{1,0:T(8,128)(2,1)S(1)}, bf16[1024,128]{1,0:T(8,128)(2,1)S(1)}) custom-call(s32[1]{0:T(128)} %bitcast.me, s32[1]{0:T(128)} %bitcast.3.mine, bf16[2048,1536]{1,0:T(8,128)(2,1)S(1)} %bitcast.5, bf16[64,1536]{1,0:T(8,128)(2,1)S(1)} %shard_map.77.rest_1_, bf16[64,1536]{1,0:T(8,128)(2,1)} %collective-permute-done.20.rest_2_), custom_call_target="tpu_custom_call" | custom-call | tf_op jit(solution)/shard_map/pallas_call | solution.py:28
  73.3 0.0 collective-permute-done.12.rest_4_
  73.3 0.6 collective-permute-start.21
  73.9 6.5 %shard_map.70.rest_6_ = f32[768,12288]{1,0:T(8,128)} custom-call(s32[1]{0:T(128)} %bitcast.me, bf16[768,256]{1,0:T(8,128)(2,1)S(1)} %get-tuple-element.12.rest_0_, bf16[256,768]{1,0:T(8,128)(2,1)S(1)} %copy-done.7, bf16[256,768]{1,0:T(8,128)(2,1)S(1)} %copy-done.11, bf16[256,768]{1,0:T(8,128)(2,1)S(1)} %copy-done.5, ...), custom_call_target="tpu_custom_call", output_to_operand_aliasing={{}: (7, {})} | custom-call | flops 1207959552 | tf_op jit(solution)/shard_map/pallas_call | solution.py:28
  80.5 0.0 collective-permute-done.11.rest_2_
  80.5 7.9 %shard_map.71.rest_6_ = f32[768,12288]{1,0:T(8,128)} custom-call(s32[1]{0:T(128)} %bitcast.me, bf16[768,256]{1,0:T(8,128)(2,1)S(1)} %get-tuple-element.12.rest_0_, bf16[256,768]{1,0:T(8,128)(2,1)} %collective-permute-done.10.rest_1_, bf16[256,768]{1,0:T(8,128)(2,1)} %collective-permute-done.11.rest_2_, ...), custom_call_target="tpu_custom_call", output_to_operand_aliasing={{}: (7, {})} | custom-call | flops 1207959552 | tf_op jit(solution)/shard_map/pallas_call | solution.py:28
  88.4 0.0 collective-permute-done.9.rest_4_
  88.4 0.0 collective-permute-done.8.rest_2_
  88.4 7.9 %shard_map.72.rest_4_ = f32[768,12288]{1,0:T(8,128)} custom-call(s32[1]{0:T(128)} %bitcast.me, bf16[768,256]{1,0:T(8,128)(2,1)S(1)} %get-tuple-element.12.rest_0_, bf16[256,768]{1,0:T(8,128)(2,1)} %collective-permute-done.7.rest_1_, bf16[256,768]{1,0:T(8,128)(2,1)} %collective-permute-done.8.rest_2_, ...), custom_call_target="tpu_custom_call", output_to_operand_aliasing={{}: (7, {})} | custom-call | flops 1207959552 | tf_op jit(solution)/shard_map/pallas_call | solution.py:28
  96.3 0.0 collective-permute-done.4.rest_2_
  96.3 0.0 collective-permute-done.21.rest_7_
  96.3 4.1 %shard_map.79 = (f32[768,12288]{1,0:T(8,128)}, f32[1024,128]{1,0:T(8,128)}) custom-call(s32[1]{0:T(128)} %bitcast.me, bf16[768,256]{1,0:T(8,128)(2,1)S(1)} %get-tuple-element.12.rest_0_, bf16[256,768]{1,0:T(8,128)(2,1)S(1)} %collective-permute-done.3.rest_1_, bf16[256,768]{1,0:T(8,128)(2,1)S(1)} %collective-permute-done.4.rest_2_, ...), custom_call_target="tpu_custom_call", output_to_operand_aliasing={{0}: (5, {})} | custom-call | flops 603979776 | tf_op jit(solution)/shard_map/pallas_call | solution.py:28
  (23 shorter events, 0.1 us)
Async XLA Ops:
  0.6 12.4 %collective-permute-start = (bf16[256,768]{1,0:T(8,128)(2,1)}, bf16[256,768]{1,0:T(8,128)(2,1)S(1)}, u32[]{:S(2)}, u32[]{:S(2)}) collective-permute-start(bf16[256,768]{1,0:T(8,128)(2,1)} %bitcast.6), channel_id=1, source_target_pairs={{0,1},{1,0},{2,3},{3,2},{4,5},{5,4},{6,7},{7,6},{8,9},{9,8},{10,11... | collective-permute-start | bytes 1179656 | tf_op jit(solution)/shard_map/ppermute | solution.py:336
  3.7 14.0 %collective-permute-start.5 = (bf16[256,768]{1,0:T(8,128)(2,1)}, bf16[256,768]{1,0:T(8,128)(2,1)S(1)}, u32[]{:S(2)}, u32[]{:S(2)}) collective-permute-start(bf16[256,768]{1,0:T(8,128)(2,1)} %bitcast.7), channel_id=1, source_target_pairs={{0,8},{2,10},{4,12},{6,14},{8,16},{10,18},{12,20},{14,22},{16,24},... | collective-permute-start | bytes 1179656 | tf_op jit(solution)/shard_map/ppermute | solution.py:314
  5.2 12.4 %collective-permute-start.1 = (bf16[256,768]{1,0:T(8,128)(2,1)}, bf16[256,768]{1,0:T(8,128)(2,1)S(1)}, u32[]{:S(2)}, u32[]{:S(2)}) collective-permute-start(bf16[256,768]{1,0:T(8,128)(2,1)} %bitcast.8), channel_id=1, source_target_pairs={{0,2},{2,0},{4,6},{6,4},{8,10},{10,8},{12,14},{14,12},{16,18},{18,... | collective-permute-start | bytes 1179656 | tf_op jit(solution)/shard_map/ppermute | solution.py:314
  5.2 0.7 copy-start.12
  8.1 2.0 %collective-permute-start.16 = (bf16[64,1536]{1,0:T(8,128)(2,1)S(1)}, bf16[64,1536]{1,0:T(8,128)(2,1)S(1)}, u32[]{:S(2)}, u32[]{:S(2)}) collective-permute-start(bf16[64,1536]{1,0:T(8,128)(2,1)S(1)} %get-tuple-element.15), channel_id=1, source_target_pairs={{0,2},{2,0},{4,6},{6,4},{8,10},{10,8},{12,14},{14,12},{16,18},{18,... | collective-permute-start | bytes 589832 | tf_op jit(solution)/shard_map/ppermute | solution.py:314
  8.8 16.8 %collective-permute-start.13 = (bf16[256,768]{1,0:T(8,128)(2,1)}, bf16[256,768]{1,0:T(8,128)(2,1)S(1)}, u32[]{:S(2)}, u32[]{:S(2)}) collective-permute-start(bf16[256,768]{1,0:T(8,128)(2,1)} %bitcast.9), channel_id=1, source_target_pairs={{0,4},{2,6},{4,0},{6,2},{8,12},{10,14},{12,8},{14,10},{16,20},{18,... | collective-permute-start | bytes 1179656 | tf_op jit(solution)/shard_map/ppermute | solution.py:314
  10.1 17.3 %collective-permute-start.2 = (bf16[256,768]{1,0:T(8,128)(2,1)}, bf16[256,768]{1,0:T(8,128)(2,1)}, u32[]{:S(2)}, u32[]{:S(2)}) collective-permute-start(bf16[256,768]{1,0:T(8,128)(2,1)} %bitcast.10), channel_id=1, source_target_pairs={{0,24},{2,26},{4,28},{6,30},{8,0},{10,2},{12,4},{14,6},{16,8},{18,... | collective-permute-start | bytes 1179656 | tf_op jit(solution)/shard_map/ppermute | solution.py:314
  13.0 11.3 %collective-permute-start.17 = (bf16[64,1536]{1,0:T(8,128)(2,1)S(1)}, bf16[64,1536]{1,0:T(8,128)(2,1)S(1)}, u32[]{:S(2)}, u32[]{:S(2)}) collective-permute-start(bf16[64,1536]{1,0:T(8,128)(2,1)S(1)} %shard_map.74.a), channel_id=1, source_target_pairs={{0,4},{2,6},{4,0},{6,2},{8,12},{10,14},{12,8},{14,10},{16,20},{18,... | collective-permute-start | bytes 589832 | tf_op jit(solution)/shard_map/ppermute | solution.py:314
  17.6 39.5 %copy-start.4 = (bf16[256,768]{1,0:T(8,128)(2,1)}, bf16[256,768]{1,0:T(8,128)(2,1)S(1)}, u32[]{:S(2)}) copy-start(bf16[256,768]{1,0:T(8,128)(2,1)S(1)} %collective-permute-done.5.rest_3_) | copy-start | bytes 1179652
  17.6 21.3 %collective-permute-start.6 = (bf16[256,768]{1,0:T(8,128)(2,1)S(1)}, bf16[256,768]{1,0:T(8,128)(2,1)}, u32[]{:S(2)}, u32[]{:S(2)}) collective-permute-start(bf16[256,768]{1,0:T(8,128)(2,1)S(1)} %collective-permute-done.5.rest_3_), channel_id=1, source_target_pairs={{0,8},{2,10},{4,12},{6,14},{8,16},{10,18},{12,20},{14,22},{16,24},... | collective-permute-start | bytes 1179656 | tf_op jit(solution)/shard_map/ppermute | solution.py:314
  17.7 21.8 %collective-permute-start.15 = (bf16[256,768]{1,0:T(8,128)(2,1)S(1)}, bf16[256,768]{1,0:T(8,128)(2,1)S(1)}, u32[]{:S(2)}, u32[]{:S(2)}) collective-permute-start(bf16[256,768]{1,0:T(8,128)(2,1)S(1)} %collective-permute-done.5.rest_3_), channel_id=1, source_target_pairs={{0,2},{2,0},{4,6},{6,4},{8,10},{10,8},{12,14},{14,12},{16,18},{18,... | collective-permute-start | bytes 1179656 | tf_op jit(solution)/shard_map/ppermute | solution.py:314
  24.3 15.8 %collective-permute-start.10 = (bf16[256,768]{1,0:T(8,128)(2,1)S(1)}, bf16[256,768]{1,0:T(8,128)(2,1)}, u32[]{:S(2)}, u32[]{:S(2)}) collective-permute-start(bf16[256,768]{1,0:T(8,128)(2,1)S(1)} %collective-permute-done.5.rest_3_), channel_id=1, source_target_pairs={{0,4},{2,6},{4,0},{6,2},{8,12},{10,14},{12,8},{14,10},{16,20},{18,... | collective-permute-start | bytes 1179656 | tf_op jit(solution)/shard_map/ppermute | solution.py:314
  25.7 31.5 %copy-start.6 = (bf16[256,768]{1,0:T(8,128)(2,1)}, bf16[256,768]{1,0:T(8,128)(2,1)S(1)}, u32[]{:S(2)}) copy-start(bf16[256,768]{1,0:T(8,128)(2,1)S(1)} %collective-permute-done.13.rest_1_) | copy-start | bytes 1179652
  25.7 11.7 %collective-permute-start.18 = (bf16[64,1536]{1,0:T(8,128)(2,1)S(1)}, bf16[64,1536]{1,0:T(8,128)(2,1)S(1)}, u32[]{:S(2)}, u32[]{:S(2)}) collective-permute-start(bf16[64,1536]{1,0:T(8,128)(2,1)S(1)} %shard_map.75.a), channel_id=1, source_target_pairs={{0,8},{2,10},{4,12},{6,14},{8,0},{10,2},{12,4},{14,6},{16,24},{18,... | collective-permute-start | bytes 589832 | tf_op jit(solution)/shard_map/ppermute | solution.py:317
  27.4 22.6 %collective-permute-start.14 = (bf16[256,768]{1,0:T(8,128)(2,1)S(1)}, bf16[256,768]{1,0:T(8,128)(2,1)S(1)}, u32[]{:S(2)}, u32[]{:S(2)}) collective-permute-start(bf16[256,768]{1,0:T(8,128)(2,1)S(1)} %collective-permute-done.13.rest_1_), channel_id=1, source_target_pairs={{0,2},{2,0},{4,6},{6,4},{8,10},{10,8},{12,14},{14,12},{16,18},{18,... | collective-permute-start | bytes 1179656 | tf_op jit(solution)/shard_map/ppermute | solution.py:314
  37.4 13.8 %collective-permute-start.3 = (bf16[256,768]{1,0:T(8,128)(2,1)}, bf16[256,768]{1,0:T(8,128)(2,1)S(1)}, u32[]{:S(2)}, u32[]{:S(2)}) collective-permute-start(bf16[256,768]{1,0:T(8,128)(2,1)} %collective-permute-done.2.rest_3_), channel_id=1, source_target_pairs={{0,4},{2,6},{4,0},{6,2},{8,12},{10,14},{12,8},{14,10},{16,20},{18,... | collective-permute-start | bytes 1179656 | tf_op jit(solution)/shard_map/ppermute | solution.py:314
  38.9 18.3 %collective-permute-start.7 = (bf16[256,768]{1,0:T(8,128)(2,1)}, bf16[256,768]{1,0:T(8,128)(2,1)}, u32[]{:S(2)}, u32[]{:S(2)}) collective-permute-start(bf16[256,768]{1,0:T(8,128)(2,1)} %collective-permute-done.6.rest_3_), channel_id=1, source_target_pairs={{0,4},{2,6},{4,0},{6,2},{8,12},{10,14},{12,8},{14,10},{16,20},{18,... | collective-permute-start | bytes 1179656 | tf_op jit(solution)/shard_map/ppermute | solution.py:314
  39.5 17.7 %copy-start.8 = (bf16[256,768]{1,0:T(8,128)(2,1)}, bf16[256,768]{1,0:T(8,128)(2,1)S(1)}, u32[]{:S(2)}) copy-start(bf16[256,768]{1,0:T(8,128)(2,1)S(1)} %collective-permute-done.15.rest_4_) | copy-start | bytes 1179652
  39.5 10.4 %collective-permute-start.19 = (bf16[64,1536]{1,0:T(8,128)(2,1)S(1)}, bf16[64,1536]{1,0:T(8,128)(2,1)S(1)}, u32[]{:S(2)}, u32[]{:S(2)}) collective-permute-start(bf16[64,1536]{1,0:T(8,128)(2,1)S(1)} %shard_map.76.a), channel_id=1, source_target_pairs={{0,16},{2,18},{4,20},{6,22},{8,24},{10,26},{12,28},{14,30},{16,0},... | collective-permute-start | bytes 589832 | tf_op jit(solution)/shard_map/ppermute | solution.py:317
  40.1 33.2 %collective-permute-start.12 = (bf16[256,768]{1,0:T(8,128)(2,1)}, bf16[256,768]{1,0:T(8,128)(2,1)}, u32[]{:S(2)}, u32[]{:S(2)}) collective-permute-start(bf16[256,768]{1,0:T(8,128)(2,1)} %collective-permute-done.6.rest_3_), channel_id=1, source_target_pairs={{0,2},{2,0},{4,6},{6,4},{8,10},{10,8},{12,14},{14,12},{16,18},{18,... | collective-permute-start | bytes 1179656 | tf_op jit(solution)/shard_map/ppermute | solution.py:314
  49.9 30.6 %collective-permute-start.11 = (bf16[256,768]{1,0:T(8,128)(2,1)}, bf16[256,768]{1,0:T(8,128)(2,1)}, u32[]{:S(2)}, u32[]{:S(2)}) collective-permute-start(bf16[256,768]{1,0:T(8,128)(2,1)} %collective-permute-done.10.rest_1_), channel_id=1, source_target_pairs={{0,2},{2,0},{4,6},{6,4},{8,10},{10,8},{12,14},{14,12},{16,18},{18,... | collective-permute-start | bytes 1179656 | tf_op jit(solution)/shard_map/ppermute | solution.py:314
  50.0 0.8 copy-start.10
  50.7 12.1 %collective-permute-start.20 = (bf16[64,1536]{1,0:T(8,128)(2,1)S(1)}, bf16[64,1536]{1,0:T(8,128)(2,1)}, u32[]{:S(2)}, u32[]{:S(2)}) collective-permute-start(bf16[64,1536]{1,0:T(8,128)(2,1)S(1)} %shard_map.77.rest_1_), channel_id=1, source_target_pairs={{0,2},{2,0},{4,6},{6,4},{8,10},{10,8},{12,14},{14,12},{16,18},{18,... | collective-permute-start | bytes 589832 | tf_op jit(solution)/shard_map/ppermute | solution.py:314
  51.2 37.2 %collective-permute-start.9 = (bf16[256,768]{1,0:T(8,128)(2,1)}, bf16[256,768]{1,0:T(8,128)(2,1)}, u32[]{:S(2)}, u32[]{:S(2)}) collective-permute-start(bf16[256,768]{1,0:T(8,128)(2,1)} %collective-permute-done.2.rest_3_), channel_id=1, source_target_pairs={{0,2},{2,0},{4,6},{6,4},{8,10},{10,8},{12,14},{14,12},{16,18},{18,... | collective-permute-start | bytes 1179656 | tf_op jit(solution)/shard_map/ppermute | solution.py:314
  57.2 31.2 %collective-permute-start.8 = (bf16[256,768]{1,0:T(8,128)(2,1)}, bf16[256,768]{1,0:T(8,128)(2,1)}, u32[]{:S(2)}, u32[]{:S(2)}) collective-permute-start(bf16[256,768]{1,0:T(8,128)(2,1)} %collective-permute-done.7.rest_1_), channel_id=1, source_target_pairs={{0,2},{2,0},{4,6},{6,4},{8,10},{10,8},{12,14},{14,12},{16,18},{18,... | collective-permute-start | bytes 1179656 | tf_op jit(solution)/shard_map/ppermute | solution.py:314
  57.2 12.4 %slice-start = ((s8[6291456]{0:T(1024)(128)(4,1)}), s8[2097152]{0:T(1024)(128)(4,1)S(1)}, s32[]{:S(2)}) async-start(s8[6291456]{0:T(1024)(128)(4,1)} %bitcast.4), calls=%async_computation | async-start | bytes 4194304
  59.9 2.2 %copy-start = (f32[4,384,768]{2,1,0:T(8,128)}, f32[4,384,768]{2,1,0:T(8,128)S(1)}, u32[]{:S(2)}) copy-start(f32[4,384,768]{2,1,0:T(8,128)S(1)} %get-tuple-element.10.rest_0_) | copy-start | bytes 14155780
  62.1 0.7 copy-start.2
  62.8 33.4 %collective-permute-start.4 = (bf16[256,768]{1,0:T(8,128)(2,1)S(1)}, bf16[256,768]{1,0:T(8,128)(2,1)S(1)}, u32[]{:S(2)}, u32[]{:S(2)}) collective-permute-start(bf16[256,768]{1,0:T(8,128)(2,1)S(1)} %collective-permute-done.3.rest_1_), channel_id=1, source_target_pairs={{0,2},{2,0},{4,6},{6,4},{8,10},{10,8},{12,14},{14,12},{16,18},{18,... | collective-permute-start | bytes 1179656 | tf_op jit(solution)/shard_map/ppermute | solution.py:314
  63.3 2.3 %copy-start.1 = (f32[4,384,768]{2,1,0:T(8,128)S(1)}, f32[4,384,768]{2,1,0:T(8,128)}, u32[]{:S(2)}) copy-start(f32[4,384,768]{2,1,0:T(8,128)} %copy-done) | copy-start | bytes 14155780
  65.7 1.0 copy-start.3
  66.7 3.9 %slice-start.1 = ((s8[6291456]{0:T(1024)(128)(4,1)}), s8[4194304]{0:T(1024)(128)(4,1)S(1)}, s32[]{:S(2)}) async-start(s8[6291456]{0:T(1024)(128)(4,1)} %bitcast.4), calls=%async_computation.1 | async-start | bytes 8388608
  66.7 7.2 %copy-start.5 = (bf16[256,768]{1,0:T(8,128)(2,1)S(1)}, bf16[256,768]{1,0:T(8,128)(2,1)}, u32[]{:S(2)}) copy-start(bf16[256,768]{1,0:T(8,128)(2,1)} %copy-done.4) | copy-start | bytes 1179652
  66.7 7.2 %copy-start.7 = (bf16[256,768]{1,0:T(8,128)(2,1)S(1)}, bf16[256,768]{1,0:T(8,128)(2,1)}, u32[]{:S(2)}) copy-start(bf16[256,768]{1,0:T(8,128)(2,1)} %copy-done.6) | copy-start | bytes 1179652
  66.7 7.2 %copy-start.9 = (bf16[256,768]{1,0:T(8,128)(2,1)S(1)}, bf16[256,768]{1,0:T(8,128)(2,1)}, u32[]{:S(2)}) copy-start(bf16[256,768]{1,0:T(8,128)(2,1)} %copy-done.8) | copy-start | bytes 1179652
  66.7 7.2 %copy-start.11 = (bf16[256,768]{1,0:T(8,128)(2,1)S(1)}, bf16[256,768]{1,0:T(8,128)(2,1)}, u32[]{:S(2)}) copy-start(bf16[256,768]{1,0:T(8,128)(2,1)} %copy-done.10) | copy-start | bytes 1179652
  73.3 23.0 %collective-permute-start.21 = (bf16[1024,128]{1,0:T(8,128)(2,1)S(1)}, bf16[1024,128]{1,0:T(8,128)(2,1)S(1)}, u32[]{:S(2)}, u32[]{:S(2)}) collective-permute-start(bf16[1024,128]{1,0:T(8,128)(2,1)S(1)} %get-tuple-element.17), channel_id=1, source_target_pairs={{0,1},{1,0},{2,3},{3,2},{4,5},{5,4},{6,7},{7,6},{8,9},{9,8},{10,11... | collective-permute-start | bytes 786440 | tf_op jit(solution)/shard_map/ppermute | solution.py:378
